TPU v7x, 32 devices: a whole 2x2x4 slice. The times are simulated.
32 devices in a mesh: gx: 4 (over x, core), gy: 2 (over y), gz: 4 (over z).
Axes of the slice: x: 2, y: 2, z: 4, core: 2. Of those that a mesh axis runs over, the one named last changes fastest.
Arguments:
- start_field: float32 [256, 128, 1024], P('gx', 'gy', 'gz'), may hold values from -6 to 6
- right_side: float32 [256, 128, 1024], P('gx', 'gy', 'gz'), may hold values from -6 to 6
Outputs:
- corrected: float32 [256, 128, 1024], P('gx', 'gy', 'gz')
All inputs are finite; a program needn't handle non-finite values.
Results may differ from a plain program's by a relative error of at most 0.00002.
Values sent between devices are 32-bit elements; how exact they have to be, the bound alone decides.
A program may use at most 128 MiB of HBM per device.

v0:
```python
import functools

import jax
import jax.numpy as jnp
from jax import lax
from jax.experimental import pallas as pl
from jax.experimental.pallas import tpu as pltpu
from jax.sharding import PartitionSpec as P

FINE_SWEEPS = 2
COARSE_SWEEPS = 4
OMEGA = 6.0 / 7.0
STEP = OMEGA / 1.5
LANES = 128
PAD = 8
ROWS = 16
AXES = ("gx", "gy", "gz")
MESH = pl.DeviceIdType.MESH

FACES = ((1, 0, 0), (-1, 0, 0), (0, 1, 0), (0, -1, 0), (0, 0, 1), (0, 0, -1))
EDGES = ((0, 1, 1), (1, 1, 0), (1, 0, 1), (1, 1, 1))
NEIGHBOURS = FACES + EDGES + tuple(tuple(-c for c in d) for d in EDGES)
N_COPIES = 10 * (FINE_SWEEPS + 1) + 4 + 6 * (COARSE_SWEEPS - 1) + 7


def rotated(values, shift):
    return pltpu.roll(values, shift, 1)


def split_dot(values, matrix):
    high = values.astype(jnp.bfloat16)
    rest = values - high.astype(jnp.float32)
    middle = rest.astype(jnp.bfloat16)
    low = (rest - middle.astype(jnp.float32)).astype(jnp.bfloat16)
    total = jnp.dot(low, matrix, preferred_element_type=jnp.float32)
    total = total + jnp.dot(middle, matrix, preferred_element_type=jnp.float32)
    return total + jnp.dot(high, matrix, preferred_element_type=jnp.float32)


def correct_kernel(
    sizes, start_hbm, right_hbm, u2, q_ref,
    u0, u1, f, ys, yr, zs, zr, zm, rk, rs, rr, px, py, rys, ryr, rdr, rzs, rzr, rhs,
    c0, c1, c2, c3, cys, cyr, czs, czr, czm, xyr, xzr, yzr, xyzr, ze,
    local_sem, send_sem, recv_sem,
):
    nt, nx, ny, _ = f.shape
    mx, my = nx // 2, ny // 2
    half = nx // 2
    me = tuple(lax.axis_index(a) for a in AXES)

    def lanes(rows):
        return lax.broadcasted_iota(jnp.int32, (rows, LANES), 1)

    lane, lane_c = lanes(ny), lanes(my)

    def there(d):
        found = None
        for at, step, size in zip(me, d, sizes):
            if step:
                one = at < size - 1 if step > 0 else at > 0
                found = one if found is None else jnp.logical_and(found, one)
        return found

    def minus(d):
        return tuple(-c for c in d)

    def device(d):
        return tuple(at + step for at, step in zip(me, d))

    sent = []

    def send(src, dst, d):
        number = len(sent)

        def copy(to):
            return pltpu.make_async_remote_copy(
                src_ref=src, dst_ref=dst, send_sem=send_sem.at[number],
                recv_sem=recv_sem.at[number], device_id=device(to), device_id_type=MESH)

        @pl.when(there(d))
        def _():
            copy(d).start()

        sent.append((copy, d, dst))
        return number

    def arrive(number):
        copy, d, dst = sent[number]

        @pl.when(there(minus(d)))
        def _():
            copy(minus(d)).wait_recv()

        @pl.when(jnp.logical_not(there(minus(d))))
        def _():
            dst[...] = jnp.zeros(dst.shape, dst.dtype)

    loads = []
    for into, source in ((u0, start_hbm), (f, right_hbm)):
        for h in range(2):
            for t in range(nt):
                rows = pl.ds(h * half, half)
                to = f.at[t, rows] if into is f else u0.at[t, pl.ds(1 + h * half, half), pl.ds(PAD, ny), :]
                loads.append(pltpu.make_async_copy(
                    source.at[rows, :, pl.ds(t * LANES, LANES)], to, local_sem.at[len(loads)]))
    for load in loads:
        load.start()

    barrier = pltpu.get_barrier_semaphore()
    expected = jnp.int32(0)
    for d in NEIGHBOURS:
        @pl.when(there(d))
        def _():
            pl.semaphore_signal(barrier, inc=1, device_id=device(d), device_id_type=MESH)
        expected = expected + there(d).astype(jnp.int32)
    zs[...] = jnp.zeros(zs.shape, zs.dtype)
    czs[...] = jnp.zeros(czs.shape, czs.dtype)
    pl.semaphore_wait(barrier, expected)

    mid = pl.ds(PAD, ny)

    def pack_lanes(ref, at, place, first, last):
        index = lanes(first.shape[0])
        both = rotated(jnp.where(index == LANES - 1, last, first), 2 * place + 1)
        chosen = jnp.logical_or(index == 2 * place, index == 2 * place + 1)
        ref[at] = jnp.where(chosen, both, ref[at])

    def merge_lanes(low, high):
        index = lanes(low.shape[0])
        return jnp.where(lax.rem(index, 2) == 0, low, rotated(high, LANES - 2))

    block = ROWS if ny % ROWS == 0 else ny
    blocks = range(0, ny, block)

    def pack_fine(k, h, x, row, planes):
        for t in range(nt):
            if row == 0:
                ys[k, 0, t, pl.ds(x, 1), :] = planes[t][0:1, :]
            if row == ny - block:
                ys[k, 1, t, pl.ds(x, 1), :] = planes[t][block - 1:block, :]
        pack_lanes(zs, (k, h, pl.ds(row, block)), x - h * half, planes[0], planes[nt - 1])

    def send_low(u):
        return send(u.at[:, 1, mid, :], u.at[:, nx + 1, mid, :], (-1, 0, 0))

    def send_high(u):
        return send(u.at[:, nx, mid, :], u.at[:, 0, mid, :], (1, 0, 0))

    def send_yz(k, h):
        rows = pl.ds(h * half, half)
        return [
            send(ys.at[k, 1, :, rows, :], yr.at[k, 0, :, rows, :], (0, 1, 0)),
            send(ys.at[k, 0, :, rows, :], yr.at[k, 1, :, rows, :], (0, -1, 0)),
            send(zs.at[k, h], zr.at[k, h, 0], (0, 0, 1)),
            send(zs.at[k, h], zr.at[k, h, 1], (0, 0, -1)),
        ]

    def fill_fine(u, k, h, waits):
        for number in waits:
            arrive(number)
        zm[k, h] = merge_lanes(zr[k, h, 0], zr[k, h, 1])

        def rows(x, _):
            for t in range(nt):
                u[t, x + 1, PAD - 1:PAD, :] = yr[k, 0, t, pl.ds(x, 1), :]
                u[t, x + 1, PAD + ny:PAD + ny + 1, :] = yr[k, 1, t, pl.ds(x, 1), :]
            return 0
        lax.fori_loop(h * half, (h + 1) * half, rows, 0, unroll=4)

    lane_b = lanes(block)

    def around(u, k, h, x, row):
        sums = []
        outer = rotated(zm[k, h, pl.ds(row, block), :], lax.rem(LANES - 2 * (x - h * half), LANES))
        here = pl.ds(PAD + row, block)
        planes = [u[t, x + 1, here, :] for t in range(nt)]
        left = [rotated(p, 1) for p in planes]
        right = [rotated(p, LANES - 1) for p in planes]
        for t in range(nt):
            before = jnp.where(lane_b == 0, left[t - 1] if t else outer, left[t])
            after = jnp.where(lane_b == LANES - 1, right[t + 1] if t < nt - 1 else outer, right[t])
            total = u[t, x, here, :] + u[t, x + 2, here, :]
            total = total + u[t, x + 1, pl.ds(PAD - 1 + row, block), :]
            total = total + u[t, x + 1, pl.ds(PAD + 1 + row, block), :]
            sums.append(total + before + after)
        return planes, sums

    waits_yz, low_arrival, high_arrival = [None, None], None, None
    for h in range(2):
        for load in loads[h * nt:(h + 1) * nt]:
            load.wait()

        def pack_start(j, _, h=h):
            for x in (2 * j, 2 * j + 1):
                for row in blocks:
                    pack_fine(0, h, x, row, [u0[t, x + 1, pl.ds(PAD + row, block), :] for t in range(nt)])
            return 0

        lax.fori_loop(h * half // 2, (h + 1) * half // 2, pack_start, 0)
        waits_yz[h] = send_yz(0, h)
        if h == 0:
            high_arrival = send_low(u0)
        else:
            low_arrival = send_high(u0)
    for load in loads[2 * nt:]:
        load.wait()

    fields = (u0, u1, u2)
    for k in range(FINE_SWEEPS):
        old, new = fields[k], fields[k + 1]

        def pair(j, h, old=old, new=new, k=k):
            for row in blocks:
                for x in (2 * j, 2 * j + 1):
                    planes, sums = around(old, k, h, x, row)
                    results = []
                    for t in range(nt):
                        value = (planes[t] + f[t, x, pl.ds(row, block), :] + sums[t]) * (1.0 - OMEGA)
                        new[t, x + 1, pl.ds(PAD + row, block), :] = value
                        results.append(value)
                    pack_fine(k + 1, h, x, row, results)

        next_yz = [None, None]
        fill_fine(old, k, 0, waits_yz[0])
        lax.fori_loop(1, half // 2, lambda j, _: (pair(j, 0), 0)[1], 0)
        arrive(low_arrival)
        pair(0, 0)
        next_yz[0] = send_yz(k + 1, 0)
        next_high = send_low(new)
        arrive(high_arrival)
        fill_fine(old, k, 1, waits_yz[1])
        lax.fori_loop(half // 2, nx // 2, lambda j, _: (pair(j, 1), 0)[1], 0)
        next_yz[1] = send_yz(k + 1, 1)
        low_arrival, high_arrival = send_high(new), next_high
        waits_yz = next_yz

    smooth = fields[FINE_SWEEPS]
    k_last = FINE_SWEEPS

    def residual(x, h, row):
        planes, sums = around(smooth, k_last, h, x, row)
        return [f[t, x, pl.ds(row, block), :] - 6.0 * planes[t] + sums[t] for t in range(nt)]

    def keep(ref, row, values):
        for t in range(nt):
            ref[t, pl.ds(row, block), :] = values[t]

    def step_x(i, h, ref, out):
        for row in blocks:
            even, odd = residual(2 * i, h, row), residual(2 * i + 1, h, row)
            for t in range(nt):
                following = ref[t, pl.ds(row, block), :]
                value = 0.25 * even[t] + 0.5 * odd[t] + 0.25 * following
                px[t, i, pl.ds(row, block), :] = value
                if row == 0:
                    rys[t, pl.ds(i, 1), :] = value[0:1, :]
            keep(out, row, even)

    def start_x(x, h):
        for row in blocks:
            keep(rk, row, residual(x, h, row))

    middle = half // 2
    fill_fine(smooth, k_last, 0, waits_yz[0])
    start_x(half - 2, 0)
    lax.fori_loop(0, middle - 2, lambda j, _: (step_x(middle - 2 - j, 0, rk, rk), 0)[1], 0, unroll=2)
    arrive(low_arrival)
    step_x(0, 0, rk, rs)
    rx = send(rs, rr, (-1, 0, 0))
    arrive(high_arrival)
    fill_fine(smooth, k_last, 1, waits_yz[1])
    start_x(nx - 2, 1)
    lax.fori_loop(0, mx - 1 - middle, lambda j, _: (step_x(mx - 2 - j, 1, rk, rk), 0)[1], 0, unroll=3)
    step_x(middle - 1, 0, rk, rk)
    arrive(rx)
    step_x(mx - 1, 1, rr, rk)
    ry = send(rys, ryr, (0, -1, 0))
    rd = send(rys, rdr, (0, -1, -1))

    def weights(fine, coarse, scale):
        gap = fine - 2 * coarse
        outer = jnp.logical_or(gap == 0, gap == 2)
        value = jnp.where(gap == 1, 0.5 * scale, jnp.where(outer, 0.25 * scale, 0.0))
        return value.astype(jnp.bfloat16)

    nz = nt * LANES
    down = weights(
        lax.broadcasted_iota(jnp.int32, (nz, LANES), 0), lax.broadcasted_iota(jnp.int32, (nz, LANES), 1), 1.0)
    up = weights(
        lax.broadcasted_iota(jnp.int32, (LANES, nz), 1), lax.broadcasted_iota(jnp.int32, (LANES, nz), 0), 2.0)
    last_row = lax.broadcasted_iota(jnp.int32, (my, LANES), 0) == my - 1

    def step_y(i, pack):
        for t in range(nt):
            evens = px[t, i, pl.ds(0, my, stride=2), :]
            odds = px[t, i, pl.ds(1, my, stride=2), :]
            nexts = jnp.where(last_row, 0.0, pltpu.roll(evens, my - 1, 0))
            part = 0.25 * evens + 0.5 * odds + 0.25 * nexts
            py[i, :, t * LANES:(t + 1) * LANES] = part
            if t == 0:
                pack = jnp.where(lane_c == i, rotated(part, i), pack)
        return pack

    zero_c = jnp.zeros((my, LANES), jnp.float32)
    rzs[...] = lax.fori_loop(0, mx, step_y, zero_c, unroll=4)
    rz = send(rzs, rzr, (0, 0, -1))
    group = 4 if mx % 4 == 0 else 1

    def step_z(i, _):
        at = pl.ds(i * group, group)
        rhs[at] = split_dot(py[at].reshape(group * my, nz), down).reshape(group, my, LANES)
        return 0

    lax.fori_loop(0, mx // group, step_z, 0)

    mid_c = pl.ds(PAD, my)

    def pack_coarse(k, i, plane):
        cys[k, 0, pl.ds(i, 1), :] = plane[0:1, :]
        cys[k, 1, pl.ds(i, 1), :] = plane[my - 1:my, :]
        pack_lanes(czs, k, i, plane, plane)

    def send_coarse(c, k):
        return [
            send(c.at[mx, mid_c, :], c.at[0, mid_c, :], (1, 0, 0)),
            send(c.at[1, mid_c, :], c.at[mx + 1, mid_c, :], (-1, 0, 0)),
            send(cys.at[k, 1], cyr.at[k, 0], (0, 1, 0)),
            send(cys.at[k, 0], cyr.at[k, 1], (0, -1, 0)),
            send(czs.at[k], czr.at[k, 0], (0, 0, 1)),
            send(czs.at[k], czr.at[k, 1], (0, 0, -1)),
        ]

    for number in (ry, rd, rz):
        arrive(number)
    beyond = jnp.where(lanes(mx) == LANES - 1, 0.0625 * rotated(rdr[0], LANES - 1), 0.0)
    beyond = beyond + 0.25 * split_dot(jnp.concatenate([ryr[t] for t in range(nt)], 1), down)
    cys[0, 0] = beyond

    def finish_rhs(i, _):
        outside = 0.25 * rotated(rzr[...], LANES - 1 - i)
        value = rhs[i] + jnp.where(lane_c == LANES - 1, outside, 0.0)
        value = value + jnp.where(last_row, cys[0, 0, pl.ds(i, 1), :], 0.0)
        value = value * STEP
        rhs[i] = value
        c0[i + 1, mid_c, :] = value
        pack_coarse(0, i, value)
        return 0

    lax.fori_loop(0, mx, finish_rhs, 0, unroll=4)
    grids = (c0, c1, c2, c3)
    waits = send_coarse(c0, 0)
    for k in range(COARSE_SWEEPS - 1):
        old, new = grids[k], grids[k + 1]
        for number in waits:
            arrive(number)
        czm[k] = merge_lanes(czr[k, 0], czr[k, 1])

        def rows(i, _):
            old[i + 1, PAD - 1:PAD, :] = cyr[k, 0, pl.ds(i, 1), :]
            old[i + 1, PAD + my:PAD + my + 1, :] = cyr[k, 1, pl.ds(i, 1), :]
            return 0

        lax.fori_loop(0, mx, rows, 0, unroll=8)

        def sweep_c(i, _):
            outer = rotated(czm[k], lax.rem(LANES - 2 * i, LANES))
            plane = old[i + 1, mid_c, :]
            total = old[i, mid_c, :] + old[i + 2, mid_c, :]
            total = total + old[i + 1, PAD - 1:PAD - 1 + my, :] + old[i + 1, PAD + 1:PAD + 1 + my, :]
            total = total + jnp.where(lane_c == 0, outer, rotated(plane, 1))
            total = total + jnp.where(lane_c == LANES - 1, outer, rotated(plane, LANES - 1))
            value = (1.0 - 1.5 * STEP) * plane + rhs[i] + (0.25 * STEP) * total
            new[i + 1, mid_c, :] = value
            pack_coarse(k + 1, i, value)
            return 0

        lax.fori_loop(0, mx, sweep_c, 0, unroll=8)
        if k < COARSE_SWEEPS - 2:
            waits = send_coarse(new, k + 1)

    k = COARSE_SWEEPS - 1
    last = grids[k]
    waits = [
        send(last.at[mx, mid_c, :], last.at[0, mid_c, :], (1, 0, 0)),
        send(cys.at[k, 1], cyr.at[k, 0], (0, 1, 0)),
        send(czs.at[k], czr.at[k, 0], (0, 0, 1)),
        send(cys.at[k, 1], xyr, (1, 1, 0)),
        send(czs.at[k], xzr, (1, 0, 1)),
        send(czs.at[k], yzr, (0, 1, 1)),
        send(czs.at[k], xyzr, (1, 1, 1)),
    ]
    for number in waits:
        arrive(number)
    turn = LANES - 2 * (mx - 1)
    inside = jnp.where(lane_c == 0, rotated(xzr[...], turn), rotated(czr[k, 0], 2))
    corner = jnp.where(lane_c == 0, rotated(xyzr[...], turn), rotated(yzr[...], 2))
    ze[mid_c, :] = inside
    ze[0:PAD, :] = corner[my - PAD:my, :]
    below = jnp.zeros((PAD, LANES), jnp.float32)
    last[0, 0:PAD, :] = jnp.broadcast_to(xyr[mx - 1:mx, :], (PAD, LANES))
    last[0, PAD + my:, :] = below

    def rows_last(i, _):
        last[i + 1, 0:PAD, :] = jnp.broadcast_to(cyr[k, 0, pl.ds(i, 1), :], (PAD, LANES))
        last[i + 1, PAD + my:, :] = below
        return 0

    lax.fori_loop(0, mx, rows_last, 0, unroll=8)
    rows_e = my + 2 * PAD
    lane_e = lanes(my + PAD)
    three = 3 if (mx + 1) % 3 == 0 else 1

    def prolong_z(j, _):
        value = split_dot(last[pl.ds(j * three, three)].reshape(three * rows_e, LANES), up)
        for g in range(three):
            outside = 0.5 * rotated(ze[...], lax.rem(LANES - 2 * (j * three + g), LANES))
            for t in range(nt):
                part = value[g * rows_e:g * rows_e + my + PAD, t * LANES:(t + 1) * LANES]
                if t == 0:
                    part = part + jnp.where(lane_e == 0, outside, 0.0)
                q_ref[j * three + g, t] = part
        return 0

    lax.fori_loop(0, (mx + 1) // three, prolong_z, 0)

    for copy, d, _ in sent:
        @pl.when(there(d))
        def _():
            copy(d).wait_send()


def add_kernel(per, smooth_ref, q_ref, out_hbm, both, out_ref, sems):
    mx, nt, my = q_ref.shape[0] - 1, q_ref.shape[1], q_ref.shape[2] - PAD
    ny = 2 * my

    def spread(p, _):
        for t in range(nt):
            here = q_ref[p, t, PAD:PAD + my, :]
            before = q_ref[p, t, PAD - 1:PAD - 1 + my, :]
            both[p, t, pl.ds(0, my, stride=2), :] = 0.5 * (before + here)
            both[p, t, pl.ds(1, my, stride=2), :] = here
        return 0

    def add(j, _):
        for t in range(nt):
            part = pl.ds(t * LANES, LANES)
            here = both[j + 1, t]
            first = smooth_ref[t, 2 * j + 1, PAD:PAD + ny, :]
            second = smooth_ref[t, 2 * j + 2, PAD:PAD + ny, :]
            out_ref[2 * j, :, part] = first + 0.5 * (both[j, t] + here)
            out_ref[2 * j + 1, :, part] = second + here
        return 0

    copies = []
    spread(0, 0)
    for c in range(mx // per):
        lax.fori_loop(c * per + 1, (c + 1) * per + 1, spread, 0, unroll=2)
        lax.fori_loop(c * per, (c + 1) * per, add, 0)
        rows = pl.ds(2 * c * per, 2 * per)
        copies.append(pltpu.make_async_copy(out_ref.at[rows], out_hbm.at[rows], sems.at[c]))
        copies[-1].start()
    for copy in copies:
        copy.wait()


def on_device(sizes, start_field, right_side):
    nx, ny, nz = start_field.shape
    nt, mx, my = nz // LANES, nx // 2, ny // 2
    f32 = jnp.float32
    fine_shape = (nt, nx + 2, ny + 2 * PAD, LANES)
    fine = pltpu.VMEM(fine_shape, f32)
    coarse = pltpu.VMEM((mx + 2, my + 2 * PAD, LANES), f32)
    rounds = FINE_SWEEPS + 1
    y_faces = pltpu.VMEM((rounds, 2, nt, nx, LANES), f32)
    z_pairs = pltpu.VMEM((rounds, 2, ny, LANES), f32)
    x_plane = pltpu.VMEM((nt, ny, LANES), f32)
    y_rows = pltpu.VMEM((nt, mx, LANES), f32)
    z_pack = pltpu.VMEM((my, LANES), f32)
    vmem = pl.BlockSpec(memory_space=pltpu.VMEM)
    smooth, q = pl.pallas_call(
        functools.partial(correct_kernel, sizes),
        out_shape=(
            pltpu.VMEM(fine_shape, f32),
            pltpu.VMEM((mx + 1, nt, my + PAD, LANES), f32),
        ),
        in_specs=[pl.BlockSpec(memory_space=pltpu.HBM)] * 2,
        out_specs=(vmem, vmem),
        scratch_shapes=[
            fine, fine, pltpu.VMEM((nt, nx, ny, LANES), f32),
            y_faces, y_faces, z_pairs, pltpu.VMEM((rounds, 2, 2, ny, LANES), f32), z_pairs,
            x_plane, x_plane, x_plane, pltpu.VMEM((nt, mx, ny, LANES), f32), pltpu.VMEM((mx, my, nz), f32),
            y_rows, y_rows, y_rows, z_pack, z_pack, pltpu.VMEM((mx, my, LANES), f32),
            coarse, coarse, coarse, coarse,
            pltpu.VMEM((COARSE_SWEEPS, 2, mx, LANES), f32), pltpu.VMEM((COARSE_SWEEPS, 2, mx, LANES), f32),
            pltpu.VMEM((COARSE_SWEEPS, my, LANES), f32), pltpu.VMEM((COARSE_SWEEPS, 2, my, LANES), f32),
            pltpu.VMEM((COARSE_SWEEPS, my, LANES), f32),
            pltpu.VMEM((mx, LANES), f32), z_pack, z_pack, z_pack, pltpu.VMEM((my + PAD, LANES), f32),
            pltpu.SemaphoreType.DMA((4 * nt,)),
            pltpu.SemaphoreType.DMA((N_COPIES,)),
            pltpu.SemaphoreType.DMA((N_COPIES,)),
        ],
        compiler_params=pltpu.CompilerParams(
            collective_id=0, has_side_effects=True, vmem_limit_bytes=40 * 1024 * 1024),
    )(*(pltpu.with_memory_space_constraint(a, pltpu.HBM) for a in (start_field, right_side)))
    per = 8 if mx % 8 == 0 else 1
    return pl.pallas_call(
        functools.partial(add_kernel, per),
        out_shape=jax.ShapeDtypeStruct((nx, ny, nz), f32),
        in_specs=[vmem, vmem],
        out_specs=pl.BlockSpec(memory_space=pl.ANY),
        scratch_shapes=[
            pltpu.VMEM((mx + 1, nt, ny, LANES), f32), pltpu.VMEM((nx, ny, nz), f32),
            pltpu.SemaphoreType.DMA((mx // per,)),
        ],
        compiler_params=pltpu.CompilerParams(vmem_limit_bytes=24 * 1024 * 1024),
    )(smooth, q)


def solution(mesh):
    placed = (P(*AXES), P(*AXES))
    sizes = tuple(mesh.shape[a] for a in AXES)
    return jax.shard_map(
        functools.partial(on_device, sizes), mesh=mesh, in_specs=placed, out_specs=P(*AXES), check_vma=False
    )
```

profile of v0, /device:TPU:13, one launch (start us, length us, event | category | flops | bytes accessed | tf_op | source)
XLA Modules:
  0.0 54.2 jit_solution(15085443828647874931)
XLA Ops:
  0.0 52.0 %shard_map.28 = (f32[2,66,80,128]{3,2,1,0:T(8,128)S(1)}, f32[33,2,40,128]{3,2,1,0:T(8,128)S(1)}) custom-call(f32[64,64,256]{2,1,0:T(8,128)} %start_hbm.1, f32[64,64,256]{2,1,0:T(8,128)} %right_hbm.1), custom_call_target="tpu_custom_call" | custom-call | tf_op jit(solution)/shard_map/pallas_call | solution.py:480
  52.0 2.2 %shard_map.29 = f32[64,64,256]{2,1,0:T(8,128)} custom-call(f32[2,66,80,128]{3,2,1,0:T(8,128)S(1)} %get-tuple-element.7.smooth_ref, f32[33,2,40,128]{3,2,1,0:T(8,128)S(1)} %get-tuple-element.8.q_ref), custom_call_target="tpu_custom_call" | custom-call | tf_op jit(solution)/shard_map/pallas_call | solution.py:506
where the time goes:
time: 54.4 us; the launch traced here: 54.2 us
  Pallas kernels  54.2 us (100%)
    pallas_call x1, Pallas kernels, on_device(): pl.pallas_call(functools.partial(correct_kernel, sizes), out_shape=(pltpu...  52 us
    pallas_call x1, Pallas kernels, on_device(): pl.pallas_call(functools.partial(add_kernel, per), out_shape=jax.ShapeDty...  2.25 us

commit v1 on v0

v1 whole, which is shorter than its diff:
```python
import functools

import jax
import jax.numpy as jnp
from jax import lax
from jax.experimental import pallas as pl
from jax.experimental.pallas import tpu as pltpu
from jax.sharding import PartitionSpec as P

OMEGA = 6.0 / 7.0
SMOOTH = 1.0 - OMEGA
STEP = OMEGA / 1.5
COARSE_SWEEPS = 4
LANES = 128
PAD = 8
FX = 4
FINE_SLOT = 8
COARSE_SLOT = 16
SR = 12
AXES = ("gx", "gy", "gz")
MESH = pl.DeviceIdType.MESH
SIDES = (-1, 0, 1)
NEIGHBOURS = tuple((x, y, z) for x in SIDES for y in SIDES for z in SIDES if (x, y, z) != (0, 0, 0))
PLANAR = tuple(d for d in NEIGHBOURS if d[2] == 0)
SPILL_Z = tuple(d for d in NEIGHBOURS if d[2] and not (d[0] and d[1]))
N_COPIES = len(NEIGHBOURS) + 2 * len(PLANAR) + len(SPILL_Z)


def rotated(values, shift):
    return pltpu.roll(values, shift % LANES if isinstance(shift, int) else shift, values.ndim - 1)


def split_dot(values, matrix):
    high = values.astype(jnp.bfloat16)
    rest = values - high.astype(jnp.float32)
    middle = rest.astype(jnp.bfloat16)
    low = (rest - middle.astype(jnp.float32)).astype(jnp.bfloat16)
    total = jnp.dot(low, matrix, preferred_element_type=jnp.float32)
    total = total + jnp.dot(middle, matrix, preferred_element_type=jnp.float32)
    return total + jnp.dot(high, matrix, preferred_element_type=jnp.float32)


def fine_block(ny):
    rows = ny + PAD
    return 24 if rows % 24 == 0 else 8


def correct_kernel(
    sizes, start_hbm, right_hbm, u2, q_ref,
    u0, u1, f, px, py, e0, e1, e2, s1, s2, rs, sp, spr, fm,
    ys, yr, xr, xe, xer,
    mp, pk, em, kc, rm, rp, rpx, c0, c1, c2, c3, d0, d1, d2, d3, g0, g1, g2, ad,
    local_sem, send_sem, recv_sem,
):
    nt, nxp, nyp, _ = f.shape
    nx, ny = nxp - 2 * FX, nyp - 2 * PAD
    nz = nt * LANES
    mx, my, mz = nx // 2, ny // 2, nz // 2
    tiles = fm.shape[0]
    wide = ny + PAD
    block = fine_block(ny)
    blocks = range(0, wide, block)
    rows_c = my + PAD
    me = tuple(lax.axis_index(a) for a in AXES)
    f32 = jnp.float32

    def there(d):
        found = None
        for at, step, size in zip(me, d, sizes):
            if step:
                one = at < size - 1 if step > 0 else at > 0
                found = one if found is None else jnp.logical_and(found, one)
        return found

    def minus(d):
        return tuple(-c for c in d)

    def device(d):
        return tuple(at + step for at, step in zip(me, d))

    sent = []

    def send(src, dst, d):
        number = len(sent)

        def copy(to):
            return pltpu.make_async_remote_copy(
                src_ref=src, dst_ref=dst, send_sem=send_sem.at[number],
                recv_sem=recv_sem.at[number], device_id=device(to), device_id_type=MESH)

        @pl.when(there(d))
        def _():
            copy(d).start()

        sent.append((copy, d, dst))
        return number

    def arrive(number):
        copy, d, dst = sent[number]

        @pl.when(there(minus(d)))
        def _():
            copy(minus(d)).wait_recv()

        @pl.when(jnp.logical_not(there(minus(d))))
        def _():
            dst[...] = jnp.zeros(dst.shape, dst.dtype)

    def iota(shape, axis):
        return lax.broadcasted_iota(jnp.int32, shape, axis)

    chunks = 4 if nx % 4 == 0 else 1
    per = nx // chunks
    loads = []
    for c in range(chunks):
        for into, source in ((u0, start_hbm), (f, right_hbm)):
            for t in range(nt):
                load = pltpu.make_async_copy(
                    source.at[pl.ds(c * per, per), :, pl.ds(t * LANES, LANES)],
                    into.at[t, pl.ds(FX + c * per, per), pl.ds(PAD, ny), :], local_sem.at[len(loads)])
                load.start()
                loads.append(load)

    barrier = pltpu.get_barrier_semaphore()
    expected = jnp.int32(0)
    for d in NEIGHBOURS:
        @pl.when(there(d))
        def _(d=d):
            pl.semaphore_signal(barrier, inc=1, device_id=device(d), device_id_type=MESH)
        expected = expected + there(d).astype(jnp.int32)

    def ones(flag):
        return jnp.where(flag, 1.0, 0.0).astype(f32)

    below = tuple(ones(at > 0) for at in me)
    above = tuple(ones(at < size - 1) for at, size in zip(me, sizes))

    def inside(index, axis, length):
        return jnp.where(index < 0, below[axis], jnp.where(index >= length, above[axis], 1.0))

    edge = jnp.zeros((PAD, LANES), f32)

    def clear_rows(x, _):
        for ref in (u0, u1, u2, f):
            for t in range(nt):
                ref[t, x, 0:PAD, :] = edge
                ref[t, x, PAD + ny:, :] = edge
        return 0

    lax.fori_loop(0, nxp, clear_rows, 0)
    for ref, planes in ((u0, (-2, -1, nx, nx + 1)), (u1, (-3, -2, nx + 1, nx + 2)),
                        (u2, (-4, -3, nx + 2, nx + 3)), (f, (-3, -2, -1, nx, nx + 1, nx + 2))):
        for x in planes:
            for t in range(nt):
                ref[t, x + FX] = jnp.zeros((nyp, LANES), f32)

    def clear_px(i, _):
        for t in range(nt):
            px[t, i, 0:PAD, :] = edge
            px[t, i, PAD + ny:, :] = jnp.zeros((2 * PAD, LANES), f32)
        return 0

    lax.fori_loop(0, mx + 4, clear_px, 0)
    for ref in (e0, e1, e2):
        ref[...] = jnp.zeros(ref.shape, f32)
    for ref in (s1, s2, rs):
        for g in range(tiles):
            ref[g, 0:PAD, :] = edge
            ref[g, PAD + wide:, :] = edge
    pk[...] = jnp.zeros(pk.shape, f32)
    for ref in (c0, c1, c2, c3):
        def clear_c(i, _, ref=ref):
            ref[i, 0:PAD, :] = edge
            ref[i, PAD + rows_c:, :] = edge
            return 0
        lax.fori_loop(0, mx + PAD, clear_c, 0)
    for ref in (d0, d1, d2, d3):
        for g in range(tiles):
            ref[g, 0:PAD, :] = edge
            ref[g, PAD + rows_c:, :] = edge
    for ref in (g0, g1, g2):
        ref[...] = jnp.zeros(ref.shape, f32)
    xe[...] = jnp.zeros(xe.shape, f32)

    lane1 = iota((1, LANES), 1)

    def slots(lane, width):
        return lax.rem(lane + width // 2, LANES) // width, lax.rem(lane + width // 2, width) - width // 2

    def zinside(o, reach_low, reach_high):
        low = jnp.logical_and(o >= 0, o < reach_low)
        high = jnp.logical_and(o < 0, o >= -reach_high)
        return jnp.where(low, below[2], jnp.where(high, above[2], 0.0))

    for g in range(tiles):
        shape = (wide, LANES)
        p, o = slots(iota(shape, 1), FINE_SLOT)
        value = inside(g * 16 + p - 8, 0, nx) * inside(iota(shape, 0) - 4, 1, ny)
        fm[g] = value * zinside(o, 3, 3)
        shape = (rows_c, LANES)
        p, o = slots(iota(shape, 1), COARSE_SLOT)
        value = inside(g * 8 + p - 4, 0, mx) * inside(iota(shape, 0) - 4, 1, my)
        em[g] = value * zinside(o, 4, 3)
    kc[...] = inside(iota((rows_c, LANES), 0) - 4, 1, my)

    lane = iota((block, LANES), 1)
    slot, _ = slots(lane, FINE_SLOT)
    first_lane, last_lane = lane == 0, lane == LANES - 1
    low_half = lane < LANES // 2
    inject_1 = jnp.where(low_half, below[2], above[2]) * SMOOTH

    def row_mask(at):
        index = iota((block, LANES), 0) + (at - 4)
        if at == 0 or at + block == wide:
            return inside(index, 1, ny)
        return None

    row_masks = [row_mask(at) for at in blocks]

    def plane_mask(X):
        return inside(X - FX, 0, nx)

    def near(u, X, at, middle, before_x, after_x, inject):
        sums = []
        row = at + 4
        left = [rotated(p, 1) for p in middle]
        right = [rotated(p, LANES - 1) for p in middle]
        for t in range(nt):
            before = jnp.where(first_lane, left[t - 1] if t else inject, left[t])
            after = jnp.where(last_lane, right[t + 1] if t < nt - 1 else inject, right[t])
            total = before_x[t] + after_x[t]
            total = total + (u[t, X, pl.ds(row - 1, block), :] + u[t, X, pl.ds(row + 1, block), :])
            sums.append(total + (before + after))
        return sums

    def plane_of(u, X, at):
        return [u[t, X, pl.ds(at + 4, block), :] for t in range(nt)]

    def edges_of(planes):
        return jnp.where(low_half, planes[0], planes[nt - 1])

    def place(X):
        index = X + (8 - FX)
        return lax.div(index, 16), lax.rem(index, 16)

    def keep_edges(ref, X, at, planes):
        g, p = place(X)
        pltpu.store(
            ref.at[g, pl.ds(PAD + at, block), :], rotated(edges_of(planes), p * FINE_SLOT), mask=slot == p)

    def sweep(old, new, X0, X1, inject_of, keeps):
        for at, mask in zip(blocks, row_masks):
            def step(X, carry, at=at, mask=mask):
                before_x, middle = carry
                after_x = plane_of(old, X + 1, at)
                sums = near(old, X, at, middle, before_x, after_x, inject_of(X, at))
                factor = SMOOTH * plane_mask(X)
                if mask is not None:
                    factor = factor * mask
                results = []
                for t in range(nt):
                    value = (middle[t] + f[t, X, pl.ds(at + 4, block), :] + sums[t]) * factor
                    new[t, X, pl.ds(at + 4, block), :] = value
                    results.append(value)
                keeps(X, at, middle, results)
                return middle, after_x

            lax.fori_loop(X0, X1, step, (plane_of(old, X0 - 1, at), plane_of(old, X0, at)))

    def keeps_1(X, at, middle, results):
        keep_edges(e0, X, at, middle)
        keep_edges(e1, X, at, results)

    zero_b = jnp.zeros((block, LANES), f32)
    for c in range(chunks):
        for load in loads[c * 2 * nt:(c + 1) * 2 * nt]:
            load.wait()
        first = FX - 1 if c == 0 else FX + c * per - 1
        last = FX + nx + 1 if c == chunks - 1 else FX + (c + 1) * per - 1
        sweep(u0, u1, first, last, lambda X, at: zero_b, keeps_1)

    pl.semaphore_wait(barrier, expected)

    def inject_2(X, at):
        return edges_of(plane_of(u0, X, at)) * inject_1

    sweep(u1, u2, FX - 2, FX + nx + 2, inject_2, lambda X, at, middle, results: keep_edges(e2, X, at, results))

    def sides(ref, g, rows, width, slot_s, off, edge_ref):
        here = ref[g, rows, :]
        count = LANES // width
        zero = jnp.zeros_like(here)
        previous = rotated(ref[g - 1, rows, :], width) if g else zero
        following = rotated(ref[g + 1, rows, :], LANES - width) if g < tiles - 1 else zero
        total = jnp.where(slot_s == 0, previous, rotated(here, width))
        total = total + jnp.where(slot_s == count - 1, following, rotated(here, LANES - width))
        start, length = rows.start, rows.size
        total = total + ref[g, pl.ds(start - 1, length), :] + ref[g, pl.ds(start + 1, length), :]
        touching = edge_ref[g, rows, :]
        total = total + jnp.where(off == 0, touching, rotated(here, 1))
        total = total + jnp.where(off == -1, touching, rotated(here, LANES - 1))
        return here, total

    lane_w = iota((wide, LANES), 1)
    slot_w, off_w = slots(lane_w, FINE_SLOT)
    rows_w = pl.ds(PAD, wide)
    at_edge = jnp.where(jnp.logical_or(off_w == 0, off_w == -1), SMOOTH, 0.0)
    for g in range(tiles):
        s1[g, rows_w, :] = e0[g, rows_w, :] * fm[g] * at_edge
    for g in range(tiles):
        here, total = sides(s1, g, rows_w, FINE_SLOT, slot_w, off_w, e1)
        s2[g, rows_w, :] = (here + total) * fm[g] * SMOOTH

    for g in range(tiles):
        here = s2[g, rows_w, :]
        value = jnp.where(off_w == 0, rotated(here, 1), jnp.where(off_w == 1, rotated(here, 3), 0.0))
        value = jnp.where(off_w == -1, rotated(here, LANES - 1), value)
        sp[g, rows_w, :] = jnp.where(off_w == -2, rotated(here, LANES - 3), value)
    flat = u2.reshape(nt, nxp * nyp, LANES)

    def rows_along(y):
        return pl.ds(FX * nyp + PAD + y, nx, stride=nyp)

    for side, y in ((0, -2), (1, ny)):
        for k in range(2):
            for t in range(nt):
                ys[side, k, t] = flat[t, rows_along(y + k), :]
    corners = [d for d in PLANAR if d[0] and d[1]]
    for n, (dx, dy, _) in enumerate(corners):
        X, y = (FX + nx if dx > 0 else FX - 1), (PAD + ny if dy > 0 else PAD - 1)
        for t in range(nt):
            xe[n, t:t + 1, :] = u2[t, X, y:y + 1, :]

    def row_part(d, first, length):
        if d == 0:
            return pl.ds(first, length)
        return pl.ds(first + (length - PAD if d > 0 else 0), PAD)

    def tile_part(d):
        if d == 0:
            return pl.ds(0, tiles)
        return pl.ds(tiles - 1 if d > 0 else 0, 1)

    spill_sent = []
    for n, dx in enumerate((-1, 1)):
        source = u2.at[:, pl.ds(FX + nx if dx > 0 else FX - 2, 2), pl.ds(PAD, ny), :]
        spill_sent.append(send(source, xr.at[n], (dx, 0, 0)))
    for n, dy in enumerate((-1, 1)):
        spill_sent.append(send(ys.at[n], yr.at[n], (0, dy, 0)))
    for n, d in enumerate(corners):
        spill_sent.append(send(xe.at[n], xer.at[n], d))
    for n, (dx, dy, dz) in enumerate(SPILL_Z):
        tp, rpart = tile_part(dx), row_part(dy, 8, wide)
        source = sp.at[tp, rpart, :]
        spill_sent.append(send(source, spr.at[n, pl.ds(0, tp.size), pl.ds(0, rpart.size), :], (dx, dy, dz)))

    def residual(X, at, mask, middle, before_x, after_x):
        g, p = place(X)
        inject = rotated(s2[g, pl.ds(PAD + at, block), :], lax.rem(LANES - p * FINE_SLOT, LANES))
        sums = near(u2, X, at, middle, before_x, after_x, inject)
        factor = plane_mask(X)
        if mask is not None:
            factor = factor * mask
        return [(f[t, X, pl.ds(at + 4, block), :] - 6.0 * middle[t] + sums[t]) * factor for t in range(nt)]

    for at, mask in zip(blocks, row_masks):
        def step_x(i, carry, at=at, mask=mask):
            before_x, middle, part = carry
            X = FX + 2 * i - 3
            after_x = plane_of(u2, X + 1, at)
            beyond = plane_of(u2, X + 2, at)
            odd = residual(X, at, mask, middle, before_x, after_x)
            even = residual(X + 1, at, mask, after_x, middle, beyond)
            quarter = [0.25 * e for e in even]
            for t in range(nt):
                px[t, i, pl.ds(at + 4, block), :] = part[t] + 0.5 * odd[t] + quarter[t]
            return after_x, beyond, quarter

        start = (plane_of(u2, FX - 4, at), plane_of(u2, FX - 3, at), [zero_b] * nt)
        _, _, part = lax.fori_loop(0, mx + 3, step_x, start)
        for t in range(nt):
            px[t, mx + 3, pl.ds(at + 4, block), :] = part[t]

    for g in range(tiles):
        here, total = sides(s2, g, rows_w, FINE_SLOT, slot_w, off_w, e2)
        rs[g, rows_w, :] = (total - 6.0 * here) * fm[g]

    quarter, half = 0.25 * STEP, 0.5 * STEP

    def step_y(i, _):
        for t in range(nt):
            evens = px[t, i, pl.ds(0, rows_c, stride=2), :]
            odds = px[t, i, pl.ds(1, rows_c, stride=2), :]
            nexts = px[t, i, pl.ds(2, rows_c, stride=2), :]
            py[i, :, t * LANES:(t + 1) * LANES] = quarter * (evens + nexts) + half * odds
        return 0

    lax.fori_loop(0, mx + 4, step_y, 0)

    def weights(gap, scale):
        outer = jnp.logical_or(gap == 0, gap == 2)
        return jnp.where(gap == 1, 0.5 * scale, jnp.where(outer, 0.25 * scale, 0.0))

    def packed_index(o):
        k = jnp.where(o >= 4, mz + 3 - o, jnp.where(o >= 2, mz - 2 + o, jnp.where(o >= 0, -1 - o, mz - 1 - o)))
        return jnp.where(o <= -7, o + 6, jnp.where(jnp.logical_and(o <= -4, o >= -6), -4 - o, k))

    z_of, n_of = iota((nz, LANES), 0), iota((nz, LANES), 1)
    down = weights(z_of - 2 * n_of, 1.0)
    q_of, o_of = slots(n_of, COARSE_SLOT)
    pack_down = jnp.where(jnp.logical_and(q_of == 0, o_of != -3), weights(z_of - 2 * packed_index(o_of), 1.0), 0.0)
    down = jnp.concatenate([down, pack_down], 1).astype(jnp.bfloat16)
    k_of, n_of = iota((2 * LANES, LANES), 0), iota((2 * LANES, LANES), 1)
    over = k_of >= LANES
    p_of, of_of = slots(jnp.where(over, k_of - LANES, k_of), FINE_SLOT)
    p_of = jnp.where(over, p_of + 16, p_of)
    zf_of = jnp.where(of_of >= 0, -1 - of_of, nz - 1 - of_of)
    q_of, o_of = slots(n_of, COARSE_SLOT)
    kk_of = jnp.where(o_of == -3, mz - 1, packed_index(o_of))
    used = jnp.logical_and(of_of != 3, of_of != -4)
    pack_strip = weights(p_of - 2 * q_of, 1.0) * weights(zf_of - 2 * kk_of, 1.0)
    pack_strip = jnp.where(used, pack_strip, 0.0).astype(jnp.bfloat16)

    group = 4 if (mx + 4) % 4 == 0 else 1
    lane_c = iota((rows_c, LANES), 1)
    slot_c, off_c = slots(lane_c, COARSE_SLOT)
    rows_m = pl.ds(PAD, rows_c)

    def place_c(index):
        return lax.div(index, 8), lax.rem(index, 8)

    def step_z(j, _):
        both = split_dot(py[pl.ds(j * group, group)].reshape(group * rows_c, nz), down)
        both = both.reshape(group, rows_c, 2 * LANES)
        for n in range(group):
            index = j * group + n + 2
            mp[index, rows_m, :] = both[n, :, :LANES]
            g, q = place_c(index)
            pltpu.store(pk.at[g, rows_m, :], rotated(both[n, :, LANES:], q * COARSE_SLOT), mask=slot_c == q)
        return 0

    lax.fori_loop(0, (mx + 4) // group, step_z, 0)

    def strip_y(g):
        start = SR - 8
        evens = rs[g, pl.ds(start, rows_c, stride=2), :]
        odds = rs[g, pl.ds(start + 1, rows_c, stride=2), :]
        nexts = rs[g, pl.ds(start + 2, rows_c, stride=2), :]
        return quarter * (evens + nexts) + half * odds

    parts = [strip_y(g) for g in range(tiles)] + [jnp.zeros((rows_c, LANES), f32)]
    for g in range(tiles):
        pk[g, rows_m, :] += split_dot(jnp.concatenate(parts[g:g + 2], 1), pack_strip)

    def plane_part(dx):
        if dx == 0:
            return pl.ds(2, mx + 4)
        return pl.ds(mx, 6) if dx > 0 else pl.ds(2, 5)

    waits_m, waits_p = {}, {}
    for n, d in enumerate(PLANAR):
        planes, rows = plane_part(d[0]), row_part(d[1], PAD, rows_c)
        target = rm.at[n, pl.ds(0, planes.size), pl.ds(0, rows.size), :]
        waits_m[d] = send(mp.at[planes, rows, :], target, d)
    for n, d in enumerate(NEIGHBOURS):
        tp, rows = tile_part(d[0]), row_part(d[1], PAD, rows_c)
        if d[0] == 0:
            target = rp.at[(d[1] + 1) * 3 + d[2] + 1, :, pl.ds(0, rows.size), :]
        else:
            target = rpx.at[n, :, pl.ds(0, rows.size), :]
        waits_p[d] = send(pk.at[tp, rows, :], target, d)

    for number in spill_sent:
        arrive(number)
    lane_n = iota((ny, LANES), 1)
    _, off_n = slots(lane_n, FINE_SLOT)
    for n, X in enumerate((FX + nx - 2, FX)):
        for k in range(2):
            for t in range(nt):
                u2[t, X + k, pl.ds(PAD, ny), :] += xr[n, t, k]
    for n, y in enumerate((ny - 2, 0)):
        for k in range(2):
            for t in range(nt):
                flat[t, rows_along(y + k), :] += yr[n, k, t]
    for n, (dx, dy, _) in enumerate(corners):
        X, y = (FX if dx > 0 else FX + nx - 1), (PAD if dy > 0 else PAD + ny - 1)
        for t in range(nt):
            u2[t, X, y:y + 1, :] += xer[n, t:t + 1, :]
    at_z = {d: n for n, d in enumerate(SPILL_Z)}
    sums = {}
    for dz in (-1, 1):
        main = at_z[(0, 0, dz)]
        for dx in (-1, 1):
            spr[main, tiles - 1 if dx < 0 else 0] += spr[at_z[(dx, 0, dz)], 0]
        for dy in (-1, 1):
            row = 0 if dy > 0 else wide - PAD
            for g in range(tiles):
                spr[main, g, row:row + PAD] += spr[at_z[(0, dy, dz)], g, 0:PAD]
    for g in range(tiles):
        sp_off = off_w >= 0
        s1[g, rows_w, :] = jnp.where(sp_off, spr[at_z[(0, 0, 1)], g], spr[at_z[(0, 0, -1)], g])
    low_lanes, high_lanes = lane_n < 2, lane_n >= LANES - 2

    def add_z(x, _):
        g, p = place(x + FX)
        value = rotated(s1[g, pl.ds(SR, ny), :], lax.rem(LANES - p * FINE_SLOT, LANES))
        u2[0, x + FX, pl.ds(PAD, ny), :] += jnp.where(low_lanes, value, 0.0)
        u2[nt - 1, x + FX, pl.ds(PAD, ny), :] += jnp.where(high_lanes, value, 0.0)
        return 0

    lax.fori_loop(0, nx, add_z, 0)

    for d in PLANAR:
        arrive(waits_m[d])
    for d in NEIGHBOURS:
        arrive(waits_p[d])
    at_p = {d: n for n, d in enumerate(NEIGHBOURS)}
    at_m = {d: n for n, d in enumerate(PLANAR)}
    last = rows_c - PAD

    def row_at(dy):
        return 0 if dy > 0 else last

    pieces = {}
    for dz in SIDES:
        for g in range(tiles):
            base = pk[g, rows_m, :] if dz == 0 else rp[3 + dz + 1, g]
            pieces[dz, g] = [base[r:r + PAD] for r in range(0, rows_c, PAD)]
            for dy in (-1, 1):
                extra = rp[(dy + 1) * 3 + dz + 1, g, 0:PAD]
                pieces[dz, g][row_at(dy) // PAD] += extra
        for dx in (-1, 1):
            g = 0 if dx > 0 else tiles - 1
            for dy in SIDES:
                ref = rpx.at[at_p[(dx, dy, dz)], 0]
                if dy == 0:
                    for n in range(rows_c // PAD):
                        pieces[dz, g][n] += ref[n * PAD:(n + 1) * PAD]
                else:
                    pieces[dz, g][row_at(dy) // PAD] += ref[0:PAD]
    for g in range(tiles):
        own, low, high = (jnp.concatenate(pieces[dz, g], 0) for dz in (0, 1, -1))
        value = jnp.where(jnp.logical_and(off_c >= -2, off_c <= 1), own, 0.0)
        value = value + jnp.where(off_c >= 0, rotated(low, LANES - 4), rotated(high, 3))
        d0[g, rows_m, :] = value * em[g]
        lowest = jnp.where(jnp.logical_or(off_c == 0, off_c == 1), rotated(low, LANES - 2), 0.0)
        highest = jnp.where(jnp.logical_or(off_c == -1, off_c == -2), rotated(high, 6), 0.0)
        ad[g] = lowest + highest + jnp.where(off_c == -1, rotated(own, 2), 0.0)

    first_c, last_c = lane_c == 0, lane_c == LANES - 1
    near_c = jnp.logical_or(lane_c < 2, lane_c >= LANES - 2)

    def plane_mask_c(index):
        return inside(index - 4, 0, mx)

    def build(index, extra=None):
        g, q = place_c(index)
        here = mp[index, rows_m, :] if extra is None else extra
        value = here + jnp.where(near_c, rotated(ad[g], lax.rem(LANES - q * COARSE_SLOT, LANES)), 0.0)
        value = value * (kc[...] * plane_mask_c(index))
        c0[index, rows_m, :] = value
        pltpu.store(g0.at[g, rows_m, :], rotated(value, q * COARSE_SLOT), mask=slot_c == q)

    def rows_added(index):
        first = mp[index, pl.ds(PAD, PAD), :] + rm[at_m[(0, 1, 0)], index - 2, 0:PAD]
        middle = mp[index, pl.ds(2 * PAD, rows_c - 2 * PAD), :]
        final = mp[index, pl.ds(PAD + last, PAD), :] + rm[at_m[(0, -1, 0)], index - 2, 0:PAD]
        return jnp.concatenate([first, middle, final], 0)

    def planes_added(dx, k, own):
        value = rm[at_m[(dx, 0, 0)], k] + (own if own is not None else 0.0)
        first = value[0:PAD] + rm[at_m[(dx, 1, 0)], k, 0:PAD]
        final = value[last:] + rm[at_m[(dx, -1, 0)], k, 0:PAD]
        return jnp.concatenate([first, value[PAD:last], final], 0)

    for k in range(6):
        build(k, planes_added(1, k, rows_added(k) if k >= 2 else None))

    def build_inner(index, _):
        build(index, rows_added(index))
        return 0

    lax.fori_loop(6, mx + 2, build_inner, 0)
    for k in range(5):
        index = mx + 2 + k
        build(index, planes_added(-1, k, rows_added(index) if index < mx + 6 else None))

    grids, strips, touch = (c0, c1, c2, c3), (d0, d1, d2, d3), (g0, g1, g2)
    for k in range(COARSE_SWEEPS - 1):
        old, new = grids[k], grids[k + 1]

        def sweep_c(index, _, old=old, new=new, k=k):
            g, q = place_c(index)
            inject = rotated(strips[k][g, rows_m, :], lax.rem(LANES - q * COARSE_SLOT, LANES))
            here = old[index, rows_m, :]
            total = here + old[index - 1, rows_m, :] + old[index + 1, rows_m, :]
            total = total + old[index, pl.ds(PAD - 1, rows_c), :] + old[index, pl.ds(PAD + 1, rows_c), :]
            total = total + jnp.where(first_c, inject, rotated(here, 1))
            total = total + jnp.where(last_c, inject, rotated(here, LANES - 1))
            value = total * (kc[...] * (plane_mask_c(index) * (0.25 * STEP))) + c0[index, rows_m, :]
            new[index, rows_m, :] = value
            if k < COARSE_SWEEPS - 2:
                pltpu.store(touch[k + 1].at[g, rows_m, :], rotated(value, q * COARSE_SLOT), mask=slot_c == q)
            return 0

        lax.fori_loop(k + 1, mx + 6 - k, sweep_c, 0)
        for g in range(tiles):
            here, total = sides(strips[k], g, rows_m, COARSE_SLOT, slot_c, off_c, touch[k])
            strips[k + 1][g, rows_m, :] = (here + total) * (em[g] * (0.25 * STEP)) + d0[g, rows_m, :]

    up = weights(iota((mz, nz), 1) - 2 * iota((mz, nz), 0), 2.0).astype(jnp.bfloat16)
    three = 3 if (mx + 1) % 3 == 0 else 1

    def prolong_z(j, _):
        value = split_dot(c3[pl.ds(3 + j * three, three), rows_m, :].reshape(three * rows_c, LANES), up)
        for n in range(three):
            g, q = place_c(3 + j * three + n)
            outside = 0.5 * rotated(d3[g, rows_m, :], lax.rem(LANES - q * COARSE_SLOT, LANES))
            for t in range(nt):
                part = value[n * rows_c:(n + 1) * rows_c, t * LANES:(t + 1) * LANES]
                if t == 0:
                    part = part + jnp.where(first_c, outside, 0.0)
                q_ref[j * three + n, t] = part
        return 0

    lax.fori_loop(0, (mx + 1) // three, prolong_z, 0)

    for copy, d, _ in sent:
        @pl.when(there(d))
        def _(copy=copy, d=d):
            copy(d).wait_send()


def add_kernel(per, smooth_ref, q_ref, out_hbm, both, out_ref, sems):
    mx, nt, my = q_ref.shape[0] - 1, q_ref.shape[1], q_ref.shape[2] - PAD
    ny = 2 * my

    def spread(p, _):
        for t in range(nt):
            here = q_ref[p, t, 4:4 + my, :]
            before = q_ref[p, t, 3:3 + my, :]
            both[p, t, pl.ds(0, my, stride=2), :] = 0.5 * (before + here)
            both[p, t, pl.ds(1, my, stride=2), :] = here
        return 0

    def add(j, _):
        for t in range(nt):
            part = pl.ds(t * LANES, LANES)
            here = both[j + 1, t]
            first = smooth_ref[t, 2 * j + FX, PAD:PAD + ny, :]
            second = smooth_ref[t, 2 * j + FX + 1, PAD:PAD + ny, :]
            out_ref[2 * j, :, part] = first + 0.5 * (both[j, t] + here)
            out_ref[2 * j + 1, :, part] = second + here
        return 0

    copies = []
    spread(0, 0)
    for c in range(mx // per):
        lax.fori_loop(c * per + 1, (c + 1) * per + 1, spread, 0, unroll=2)
        lax.fori_loop(c * per, (c + 1) * per, add, 0)
        rows = pl.ds(2 * c * per, 2 * per)
        copies.append(pltpu.make_async_copy(out_ref.at[rows], out_hbm.at[rows], sems.at[c]))
        copies[-1].start()
    for copy in copies:
        copy.wait()


def on_device(sizes, start_field, right_side):
    nx, ny, nz = start_field.shape
    nt, mx, my = nz // LANES, nx // 2, ny // 2
    tiles = (nx + 16) // 16
    f32 = jnp.float32

    def vm(*shape):
        return pltpu.VMEM(shape, f32)

    fine_shape = (nt, nx + 2 * FX, ny + 2 * PAD, LANES)
    fine = vm(*fine_shape)
    strip = vm(tiles, ny + 3 * PAD, LANES)
    strip_c = vm(tiles, my + 3 * PAD, LANES)
    coarse = vm(mx + PAD, my + 3 * PAD, LANES)
    vmem = pl.BlockSpec(memory_space=pltpu.VMEM)
    smooth, q = pl.pallas_call(
        functools.partial(correct_kernel, sizes),
        out_shape=(
            pltpu.VMEM(fine_shape, f32),
            pltpu.VMEM((mx + 1, nt, my + PAD, LANES), f32),
        ),
        in_specs=[pl.BlockSpec(memory_space=pltpu.HBM)] * 2,
        out_specs=(vmem, vmem),
        scratch_shapes=[
            fine, fine, fine,
            vm(nt, mx + 4, ny + 3 * PAD, LANES), vm(mx + 4, my + PAD, nz),
            strip, strip, strip, strip, strip, strip,
            strip, vm(len(SPILL_Z), tiles, ny + PAD, LANES), vm(tiles, ny + PAD, LANES),
            vm(2, 2, nt, nx, LANES), vm(2, 2, nt, nx, LANES), vm(2, nt, 2, ny, LANES), vm(4, PAD, LANES), vm(4, PAD, LANES),
            coarse, strip_c, vm(tiles, my + PAD, LANES), vm(my + PAD, LANES),
            vm(len(PLANAR), mx + 4, my + PAD, LANES), vm(9, tiles, my + PAD, LANES),
            vm(len(NEIGHBOURS), 1, my + PAD, LANES),
            coarse, coarse, coarse, coarse, strip_c, strip_c, strip_c, strip_c, strip_c, strip_c, strip_c,
            vm(tiles, my + PAD, LANES),
            pltpu.SemaphoreType.DMA((8 * nt,)),
            pltpu.SemaphoreType.DMA((N_COPIES,)),
            pltpu.SemaphoreType.DMA((N_COPIES,)),
        ],
        compiler_params=pltpu.CompilerParams(
            collective_id=0, has_side_effects=True, vmem_limit_bytes=48 * 1024 * 1024),
    )(*(pltpu.with_memory_space_constraint(a, pltpu.HBM) for a in (start_field, right_side)))
    per = 8 if mx % 8 == 0 else 1
    return pl.pallas_call(
        functools.partial(add_kernel, per),
        out_shape=jax.ShapeDtypeStruct((nx, ny, nz), f32),
        in_specs=[vmem, vmem],
        out_specs=pl.BlockSpec(memory_space=pl.ANY),
        scratch_shapes=[
            pltpu.VMEM((mx + 1, nt, ny, LANES), f32), pltpu.VMEM((nx, ny, nz), f32),
            pltpu.SemaphoreType.DMA((mx // per,)),
        ],
        compiler_params=pltpu.CompilerParams(vmem_limit_bytes=24 * 1024 * 1024),
    )(smooth, q)


def solution(mesh):
    placed = (P(*AXES), P(*AXES))
    sizes = tuple(mesh.shape[a] for a in AXES)
    return jax.shard_map(
        functools.partial(on_device, sizes), mesh=mesh, in_specs=placed, out_specs=P(*AXES), check_vma=False
    )
```

time: 54.4 us -> 113 us (2.08)
  the two profiles are of different devices: /device:TPU:13 before, /device:TPU:0 now
where the time goes in v1:
time: 113 us
  Pallas kernels  113 us (100%)
    pallas_call x1, Pallas kernels, on_device(): pl.pallas_call(functools.partial(correct_kernel, sizes), out_shape=(pltpu...  111 us

profile of v1, /device:TPU:0, one launch (start us, length us, event | category | flops | bytes accessed | tf_op | source)
XLA Modules:
  0.0 113.2 jit_solution(14317701851725843091)
XLA Ops:
  0.0 110.9 %shard_map.28 = (f32[2,72,80,128]{3,2,1,0:T(8,128)S(1)}, f32[33,2,40,128]{3,2,1,0:T(8,128)S(1)}) custom-call(f32[64,64,256]{2,1,0:T(8,128)} %start_hbm.1, f32[64,64,256]{2,1,0:T(8,128)} %right_hbm.1), custom_call_target="tpu_custom_call" | custom-call | tf_op jit(solution)/shard_map/pallas_call | solution.py:683
  110.9 2.2 %shard_map.29 = f32[64,64,256]{2,1,0:T(8,128)} custom-call(f32[2,72,80,128]{3,2,1,0:T(8,128)S(1)} %get-tuple-element.7.smooth_ref, f32[33,2,40,128]{3,2,1,0:T(8,128)S(1)} %get-tuple-element.8.q_ref), custom_call_target="tpu_custom_call" | custom-call | tf_op jit(solution)/shard_map/pallas_call | solution.py:710

commit v2 on v1

--- a/solution.py
+++ b/solution.py
@@ -11,6 +11,10 @@
 SMOOTH = 1.0 - OMEGA
 STEP = OMEGA / 1.5
 COARSE_SWEEPS = 4
+BY = 8
+BYX = 5
+BYC = 12
+BYZ = 8
 LANES = 128
 PAD = 8
 FX = 4
@@ -38,6 +42,20 @@
     total = jnp.dot(low, matrix, preferred_element_type=jnp.float32)
     total = total + jnp.dot(middle, matrix, preferred_element_type=jnp.float32)
     return total + jnp.dot(high, matrix, preferred_element_type=jnp.float32)
+
+
+def unrolled(first, last, body, carry, by):
+    count = (last - first) // by
+
+    def several(j, carry):
+        for n in range(by):
+            carry = body(first + j * by + n, carry)
+        return carry
+
+    carry = lax.fori_loop(0, count, several, carry)
+    for index in range(first + count * by, last):
+        carry = body(index, carry)
+    return carry
 
 
 def fine_block(ny):
@@ -257,19 +275,16 @@
                 factor = SMOOTH * plane_mask(X)
                 if mask is not None:
                     factor = factor * mask
-                results = []
                 for t in range(nt):
                     value = (middle[t] + f[t, X, pl.ds(at + 4, block), :] + sums[t]) * factor
                     new[t, X, pl.ds(at + 4, block), :] = value
-                    results.append(value)
-                keeps(X, at, middle, results)
+                keeps(X, at, middle)
                 return middle, after_x
 
-            lax.fori_loop(X0, X1, step, (plane_of(old, X0 - 1, at), plane_of(old, X0, at)))
-
-    def keeps_1(X, at, middle, results):
+            unrolled(X0, X1, step, (plane_of(old, X0 - 1, at), plane_of(old, X0, at)), BY)
+
+    def keeps_1(X, at, middle):
         keep_edges(e0, X, at, middle)
-        keep_edges(e1, X, at, results)
 
     zero_b = jnp.zeros((block, LANES), f32)
     for c in range(chunks):
@@ -284,7 +299,7 @@
     def inject_2(X, at):
         return edges_of(plane_of(u0, X, at)) * inject_1
 
-    sweep(u1, u2, FX - 2, FX + nx + 2, inject_2, lambda X, at, middle, results: keep_edges(e2, X, at, results))
+    sweep(u1, u2, FX - 2, FX + nx + 2, inject_2, lambda X, at, middle: keep_edges(e1, X, at, middle))
 
     def sides(ref, g, rows, width, slot_s, off, edge_ref):
         here = ref[g, rows, :]
@@ -357,6 +372,7 @@
     def residual(X, at, mask, middle, before_x, after_x):
         g, p = place(X)
         inject = rotated(s2[g, pl.ds(PAD + at, block), :], lax.rem(LANES - p * FINE_SLOT, LANES))
+        keep_edges(e2, X, at, middle)
         sums = near(u2, X, at, middle, before_x, after_x, inject)
         factor = plane_mask(X)
         if mask is not None:
@@ -377,7 +393,7 @@
             return after_x, beyond, quarter
 
         start = (plane_of(u2, FX - 4, at), plane_of(u2, FX - 3, at), [zero_b] * nt)
-        _, _, part = lax.fori_loop(0, mx + 3, step_x, start)
+        _, _, part = unrolled(0, mx + 3, step_x, start, BYX)
         for t in range(nt):
             px[t, mx + 3, pl.ds(at + 4, block), :] = part[t]
 
@@ -395,7 +411,7 @@
             py[i, :, t * LANES:(t + 1) * LANES] = quarter * (evens + nexts) + half * odds
         return 0
 
-    lax.fori_loop(0, mx + 4, step_y, 0)
+    unrolled(0, mx + 4, step_y, 0, 4)
 
     def weights(gap, scale):
         outer = jnp.logical_or(gap == 0, gap == 2)
@@ -439,7 +455,7 @@
             pltpu.store(pk.at[g, rows_m, :], rotated(both[n, :, LANES:], q * COARSE_SLOT), mask=slot_c == q)
         return 0
 
-    lax.fori_loop(0, (mx + 4) // group, step_z, 0)
+    unrolled(0, (mx + 4) // group, step_z, 0, 3)
 
     def strip_y(g):
         start = SR - 8
@@ -508,7 +524,7 @@
         u2[nt - 1, x + FX, pl.ds(PAD, ny), :] += jnp.where(high_lanes, value, 0.0)
         return 0
 
-    lax.fori_loop(0, nx, add_z, 0)
+    unrolled(0, nx, add_z, 0, BYZ)
 
     for d in PLANAR:
         arrive(waits_m[d])
@@ -559,7 +575,6 @@
         value = here + jnp.where(near_c, rotated(ad[g], lax.rem(LANES - q * COARSE_SLOT, LANES)), 0.0)
         value = value * (kc[...] * plane_mask_c(index))
         c0[index, rows_m, :] = value
-        pltpu.store(g0.at[g, rows_m, :], rotated(value, q * COARSE_SLOT), mask=slot_c == q)
 
     def rows_added(index):
         first = mp[index, pl.ds(PAD, PAD), :] + rm[at_m[(0, 1, 0)], index - 2, 0:PAD]
@@ -580,7 +595,7 @@
         build(index, rows_added(index))
         return 0
 
-    lax.fori_loop(6, mx + 2, build_inner, 0)
+    unrolled(6, mx + 2, build_inner, 0, BYC)
     for k in range(5):
         index = mx + 2 + k
         build(index, planes_added(-1, k, rows_added(index) if index < mx + 6 else None))
@@ -599,11 +614,10 @@
             total = total + jnp.where(last_c, inject, rotated(here, LANES - 1))
             value = total * (kc[...] * (plane_mask_c(index) * (0.25 * STEP))) + c0[index, rows_m, :]
             new[index, rows_m, :] = value
-            if k < COARSE_SWEEPS - 2:
-                pltpu.store(touch[k + 1].at[g, rows_m, :], rotated(value, q * COARSE_SLOT), mask=slot_c == q)
+            pltpu.store(touch[k].at[g, rows_m, :], rotated(here, q * COARSE_SLOT), mask=slot_c == q)
             return 0
 
-        lax.fori_loop(k + 1, mx + 6 - k, sweep_c, 0)
+        unrolled(k + 1, mx + 6 - k, sweep_c, 0, BYC)
         for g in range(tiles):
             here, total = sides(strips[k], g, rows_m, COARSE_SLOT, slot_c, off_c, touch[k])
             strips[k + 1][g, rows_m, :] = (here + total) * (em[g] * (0.25 * STEP)) + d0[g, rows_m, :]
@@ -623,7 +637,7 @@
                 q_ref[j * three + n, t] = part
         return 0
 
-    lax.fori_loop(0, (mx + 1) // three, prolong_z, 0)
+    unrolled(0, (mx + 1) // three, prolong_z, 0, 3)
 
     for copy, d, _ in sent:
         @pl.when(there(d))

time: 113 us -> 38.1 us (0.34)
  Pallas kernels: 113 us -> 37.9 us
    pallas_call x1, Pallas kernels: 111 us -> 35.7 us  [on_device(): pl.pallas_call(functools.partial(correct_kernel, sizes), out_shape=(pltpu...]
where the time goes in v2:
time: 38.1 us; the launch traced here: 37.9 us
  Pallas kernels  37.9 us (99%)
    pallas_call x1, Pallas kernels, on_device(): pl.pallas_call(functools.partial(correct_kernel, sizes), out_shape=(pltpu...  35.7 us
    pallas_call x1, Pallas kernels, on_device(): pl.pallas_call(functools.partial(add_kernel, per), out_shape=jax.ShapeDty...  2.25 us

profile of v2, /device:TPU:0, one launch (start us, length us, event | category | flops | bytes accessed | tf_op | source)
XLA Modules:
  0.0 37.9 jit_solution(10928268070293551230)
XLA Ops:
  0.0 35.7 %shard_map.28 = (f32[2,72,80,128]{3,2,1,0:T(8,128)S(1)}, f32[33,2,40,128]{3,2,1,0:T(8,128)S(1)}) custom-call(f32[64,64,256]{2,1,0:T(8,128)} %start_hbm.1, f32[64,64,256]{2,1,0:T(8,128)} %right_hbm.1), custom_call_target="tpu_custom_call" | custom-call | tf_op jit(solution)/shard_map/pallas_call | solution.py:697
  35.7 2.2 %shard_map.29 = f32[64,64,256]{2,1,0:T(8,128)} custom-call(f32[2,72,80,128]{3,2,1,0:T(8,128)S(1)} %get-tuple-element.7.smooth_ref, f32[33,2,40,128]{3,2,1,0:T(8,128)S(1)} %get-tuple-element.8.q_ref), custom_call_target="tpu_custom_call" | custom-call | tf_op jit(solution)/shard_map/pallas_call | solution.py:724

commit v3 on v2

--- a/solution.py
+++ b/solution.py
@@ -11,9 +11,10 @@
 SMOOTH = 1.0 - OMEGA
 STEP = OMEGA / 1.5
 COARSE_SWEEPS = 4
-BY = 8
-BYX = 5
-BYC = 12
+BY = 20
+BYX = 14
+BYC = 40
+BYP = 3
 BYZ = 8
 LANES = 128
 PAD = 8
@@ -27,10 +28,12 @@
 NEIGHBOURS = tuple((x, y, z) for x in SIDES for y in SIDES for z in SIDES if (x, y, z) != (0, 0, 0))
 PLANAR = tuple(d for d in NEIGHBOURS if d[2] == 0)
 SPILL_Z = tuple(d for d in NEIGHBOURS if d[2] and not (d[0] and d[1]))
-N_COPIES = len(NEIGHBOURS) + 2 * len(PLANAR) + len(SPILL_Z)
+N_COPIES = 160
 
 
 def rotated(values, shift):
+    if isinstance(shift, int) and shift % LANES == 0:
+        return values
     return pltpu.roll(values, shift % LANES if isinstance(shift, int) else shift, values.ndim - 1)
 
 
@@ -44,6 +47,18 @@
     return total + jnp.dot(high, matrix, preferred_element_type=jnp.float32)
 
 
+def divide(index, by):
+    if isinstance(index, int):
+        return divmod(index, by)
+    return lax.div(index, by), lax.rem(index, by)
+
+
+def turned_back(values, shift):
+    if isinstance(shift, int):
+        return rotated(values, -shift)
+    return rotated(values, lax.rem(LANES - shift, LANES))
+
+
 def unrolled(first, last, body, carry, by):
     count = (last - first) // by
 
@@ -52,7 +67,8 @@
             carry = body(first + j * by + n, carry)
         return carry
 
-    carry = lax.fori_loop(0, count, several, carry)
+    if count:
+        carry = lax.fori_loop(0, count, several, carry)
     for index in range(first + count * by, last):
         carry = body(index, carry)
     return carry
@@ -67,7 +83,7 @@
     sizes, start_hbm, right_hbm, u2, q_ref,
     u0, u1, f, px, py, e0, e1, e2, s1, s2, rs, sp, spr, fm,
     ys, yr, xr, xe, xer,
-    mp, pk, em, kc, rm, rp, rpx, c0, c1, c2, c3, d0, d1, d2, d3, g0, g1, g2, ad,
+    mp, pk, pz, em, kc, rm, rp, rpx, c0, c1, c2, c3, d0, d1, d2, d3, g0, g1, g2, ad,
     local_sem, send_sem, recv_sem,
 ):
     nt, nxp, nyp, _ = f.shape
@@ -98,6 +114,12 @@
 
     sent = []
 
+    def by_direction(numbers):
+        found = {}
+        for number in numbers:
+            found.setdefault(sent[number][1], []).append(number)
+        return found.items()
+
     def send(src, dst, d):
         number = len(sent)
 
@@ -106,36 +128,35 @@
                 src_ref=src, dst_ref=dst, send_sem=send_sem.at[number],
                 recv_sem=recv_sem.at[number], device_id=device(to), device_id_type=MESH)
 
-        @pl.when(there(d))
-        def _():
-            copy(d).start()
-
-        sent.append((copy, d, dst))
+        sent.append((copy, d))
         return number
 
-    def arrive(number):
-        copy, d, dst = sent[number]
-
-        @pl.when(there(minus(d)))
-        def _():
-            copy(minus(d)).wait_recv()
-
-        @pl.when(jnp.logical_not(there(minus(d))))
-        def _():
-            dst[...] = jnp.zeros(dst.shape, dst.dtype)
+    def start(numbers):
+        for d, some in by_direction(numbers):
+            @pl.when(there(d))
+            def _(d=d, some=some):
+                for number in some:
+                    sent[number][0](d).start()
+
+    def arrive(numbers):
+        for d, some in by_direction(numbers):
+            @pl.when(there(minus(d)))
+            def _(d=d, some=some):
+                for number in some:
+                    sent[number][0](minus(d)).wait_recv()
 
     def iota(shape, axis):
         return lax.broadcasted_iota(jnp.int32, shape, axis)
 
-    chunks = 4 if nx % 4 == 0 else 1
-    per = nx // chunks
+    chunks = tiles - 1
+    bounds = [16 * c for c in range(tiles)]
     loads = []
-    for c in range(chunks):
+    for low, high in zip(bounds[:-1], bounds[1:]):
         for into, source in ((u0, start_hbm), (f, right_hbm)):
             for t in range(nt):
                 load = pltpu.make_async_copy(
-                    source.at[pl.ds(c * per, per), :, pl.ds(t * LANES, LANES)],
-                    into.at[t, pl.ds(FX + c * per, per), pl.ds(PAD, ny), :], local_sem.at[len(loads)])
+                    source.at[pl.ds(low, high - low), :, pl.ds(t * LANES, LANES)],
+                    into.at[t, pl.ds(FX + low, high - low), pl.ds(PAD, ny), :], local_sem.at[len(loads)])
                 load.start()
                 loads.append(load)
 
@@ -154,6 +175,8 @@
     above = tuple(ones(at < size - 1) for at, size in zip(me, sizes))
 
     def inside(index, axis, length):
+        if isinstance(index, int):
+            return below[axis] if index < 0 else above[axis] if index >= length else 1.0
         return jnp.where(index < 0, below[axis], jnp.where(index >= length, above[axis], 1.0))
 
     edge = jnp.zeros((PAD, LANES), f32)
@@ -199,6 +222,27 @@
     for ref in (g0, g1, g2):
         ref[...] = jnp.zeros(ref.shape, f32)
     xe[...] = jnp.zeros(xe.shape, f32)
+    for d in NEIGHBOURS:
+        refs = []
+        if d in PLANAR:
+            refs.append(rm.at[PLANAR.index(d)])
+        if d[0]:
+            refs.append(rpx.at[NEIGHBOURS.index(d)])
+        else:
+            refs.append(rp.at[(d[1] + 1) * 3 + d[2] + 1])
+        if d in SPILL_Z:
+            refs.append(spr.at[SPILL_Z.index(d)])
+        if d[1:] == (0, 0):
+            refs.append(xr.at[int(d[0] > 0)])
+        elif d[0] == d[2] == 0:
+            refs.append(yr.at[int(d[1] > 0)])
+        elif d in PLANAR:
+            refs.append(xer.at[[e for e in PLANAR if e[0] and e[1]].index(d)])
+
+        @pl.when(jnp.logical_not(there(minus(d))))
+        def _(refs=refs):
+            for ref in refs:
+                ref[...] = jnp.zeros(ref.shape, f32)
 
     lane1 = iota((1, LANES), 1)
 
@@ -238,19 +282,6 @@
     def plane_mask(X):
         return inside(X - FX, 0, nx)
 
-    def near(u, X, at, middle, before_x, after_x, inject):
-        sums = []
-        row = at + 4
-        left = [rotated(p, 1) for p in middle]
-        right = [rotated(p, LANES - 1) for p in middle]
-        for t in range(nt):
-            before = jnp.where(first_lane, left[t - 1] if t else inject, left[t])
-            after = jnp.where(last_lane, right[t + 1] if t < nt - 1 else inject, right[t])
-            total = before_x[t] + after_x[t]
-            total = total + (u[t, X, pl.ds(row - 1, block), :] + u[t, X, pl.ds(row + 1, block), :])
-            sums.append(total + (before + after))
-        return sums
-
     def plane_of(u, X, at):
         return [u[t, X, pl.ds(at + 4, block), :] for t in range(nt)]
 
@@ -259,47 +290,63 @@
 
     def place(X):
         index = X + (8 - FX)
-        return lax.div(index, 16), lax.rem(index, 16)
+        return divide(index, 16)
 
     def keep_edges(ref, X, at, planes):
         g, p = place(X)
         pltpu.store(
             ref.at[g, pl.ds(PAD + at, block), :], rotated(edges_of(planes), p * FINE_SLOT), mask=slot == p)
 
-    def sweep(old, new, X0, X1, inject_of, keeps):
+
+    zero_b = jnp.zeros((block, LANES), f32)
+
+    def across(u, X, at, count, inject_of):
+        planes = [plane_of(u, X + n, at) for n in range(-1, count + 1)]
+        sums = []
+        row = at + 4
+        for n in range(count):
+            middle = planes[n + 1]
+            left = [rotated(p, 1) for p in middle]
+            right = [rotated(p, LANES - 1) for p in middle]
+            inject = inject_of(X + n)
+            one = []
+            for t in range(nt):
+                before = jnp.where(first_lane, left[t - 1] if t else inject, left[t])
+                after = jnp.where(last_lane, right[t + 1] if t < nt - 1 else inject, right[t])
+                total = planes[n][t] + planes[n + 2][t]
+                total = total + (u[t, X + n, pl.ds(row - 1, block), :] + u[t, X + n, pl.ds(row + 1, block), :])
+                total = total + f[t, X + n, pl.ds(row, block), :]
+                one.append(total + (before + after))
+            sums.append(one)
+        return planes[1:-1], sums
+
+    def grouped(first, last, by, body, carry=0):
+        count = last - first
+        by = max(n for n in range(1, by + 1) if count % n == 0)
+        if count == by:
+            return body(first, by, carry)
+        return lax.fori_loop(0, count // by, lambda j, c: body(first + j * by, by, c), carry)
+
+
+    def sweep(old, new, X0, X1, keep, before=None):
         for at, mask in zip(blocks, row_masks):
-            def step(X, carry, at=at, mask=mask):
-                before_x, middle = carry
-                after_x = plane_of(old, X + 1, at)
-                sums = near(old, X, at, middle, before_x, after_x, inject_of(X, at))
-                factor = SMOOTH * plane_mask(X)
-                if mask is not None:
-                    factor = factor * mask
-                for t in range(nt):
-                    value = (middle[t] + f[t, X, pl.ds(at + 4, block), :] + sums[t]) * factor
-                    new[t, X, pl.ds(at + 4, block), :] = value
-                keeps(X, at, middle)
-                return middle, after_x
-
-            unrolled(X0, X1, step, (plane_of(old, X0 - 1, at), plane_of(old, X0, at)), BY)
-
-    def keeps_1(X, at, middle):
-        keep_edges(e0, X, at, middle)
-
-    zero_b = jnp.zeros((block, LANES), f32)
-    for c in range(chunks):
-        for load in loads[c * 2 * nt:(c + 1) * 2 * nt]:
-            load.wait()
-        first = FX - 1 if c == 0 else FX + c * per - 1
-        last = FX + nx + 1 if c == chunks - 1 else FX + (c + 1) * per - 1
-        sweep(u0, u1, first, last, lambda X, at: zero_b, keeps_1)
-
-    pl.semaphore_wait(barrier, expected)
-
-    def inject_2(X, at):
-        return edges_of(plane_of(u0, X, at)) * inject_1
-
-    sweep(u1, u2, FX - 2, FX + nx + 2, inject_2, lambda X, at, middle: keep_edges(e1, X, at, middle))
+            def step(X, by, _, at=at, mask=mask):
+                def inject_of(X):
+                    if before is None:
+                        return zero_b
+                    return edges_of(plane_of(before, X, at)) * inject_1
+
+                planes, sums = across(old, X, at, by, inject_of)
+                for n in range(by):
+                    factor = SMOOTH * plane_mask(X + n)
+                    if mask is not None:
+                        factor = factor * mask
+                    for t in range(nt):
+                        new[t, X + n, pl.ds(at + 4, block), :] = (planes[n][t] + sums[n][t]) * factor
+                    keep_edges(keep, X + n, at, planes[n])
+                return 0
+
+            grouped(X0, X1, BY, step)
 
     def sides(ref, g, rows, width, slot_s, off, edge_ref):
         here = ref[g, rows, :]
@@ -320,86 +367,95 @@
     slot_w, off_w = slots(lane_w, FINE_SLOT)
     rows_w = pl.ds(PAD, wide)
     at_edge = jnp.where(jnp.logical_or(off_w == 0, off_w == -1), SMOOTH, 0.0)
-    for g in range(tiles):
+
+    def strips_1(g):
         s1[g, rows_w, :] = e0[g, rows_w, :] * fm[g] * at_edge
-    for g in range(tiles):
+
+    def strips_2(g):
         here, total = sides(s1, g, rows_w, FINE_SLOT, slot_w, off_w, e1)
         s2[g, rows_w, :] = (here + total) * fm[g] * SMOOTH
 
-    for g in range(tiles):
+    def restrict_x(first, last, carries):
+        results = []
+        for at, mask, carry in zip(blocks, row_masks, carries):
+            def step(i, by, part, at=at, mask=mask):
+                X = FX + 2 * i - 3
+                def inject_of(X):
+                    g, p = place(X)
+                    return turned_back(s2[g, pl.ds(PAD + at, block), :], p * FINE_SLOT)
+
+                planes, sums = across(u2, X, at, 2 * by, inject_of)
+                for n in range(2 * by):
+                    keep_edges(e2, X + n, at, planes[n])
+                    for t in range(nt):
+                        sums[n][t] = sums[n][t] - 6.0 * planes[n][t]
+                for n in range(by):
+                    half_x, quarter_x = 0.5 * plane_mask(X + 2 * n), 0.25 * plane_mask(X + 2 * n + 1)
+                    quarters = [quarter_x * sums[2 * n + 1][t] for t in range(nt)]
+                    for t in range(nt):
+                        value = part[t] + half_x * sums[2 * n][t] + quarters[t]
+                        if mask is not None:
+                            value = value * mask
+                        px[t, i + n, pl.ds(at + 4, block), :] = value
+                    part = quarters
+                return part
+
+            results.append(grouped(first, last, BYX, step, carry))
+        return results
+
+    flat = u2.reshape(nt, nxp * nyp, LANES)
+
+    def rows_along(y, first, count):
+        return pl.ds((FX + first) * nyp + PAD + y, count, stride=nyp)
+
+    corners = [d for d in PLANAR if d[0] and d[1]]
+
+    def row_part(d, first, length):
+        if d == 0:
+            return pl.ds(first, length)
+        return pl.ds(first + (length - PAD if d > 0 else 0), PAD)
+
+    spill_sent, waits_m, waits_p = [], [], []
+    last_tile = tiles - 1
+
+    def pack_spill(g):
         here = s2[g, rows_w, :]
         value = jnp.where(off_w == 0, rotated(here, 1), jnp.where(off_w == 1, rotated(here, 3), 0.0))
         value = jnp.where(off_w == -1, rotated(here, LANES - 1), value)
         sp[g, rows_w, :] = jnp.where(off_w == -2, rotated(here, LANES - 3), value)
-    flat = u2.reshape(nt, nxp * nyp, LANES)
-
-    def rows_along(y):
-        return pl.ds(FX * nyp + PAD + y, nx, stride=nyp)
-
-    for side, y in ((0, -2), (1, ny)):
-        for k in range(2):
-            for t in range(nt):
-                ys[side, k, t] = flat[t, rows_along(y + k), :]
-    corners = [d for d in PLANAR if d[0] and d[1]]
-    for n, (dx, dy, _) in enumerate(corners):
-        X, y = (FX + nx if dx > 0 else FX - 1), (PAD + ny if dy > 0 else PAD - 1)
-        for t in range(nt):
-            xe[n, t:t + 1, :] = u2[t, X, y:y + 1, :]
-
-    def row_part(d, first, length):
-        if d == 0:
-            return pl.ds(first, length)
-        return pl.ds(first + (length - PAD if d > 0 else 0), PAD)
-
-    def tile_part(d):
-        if d == 0:
-            return pl.ds(0, tiles)
-        return pl.ds(tiles - 1 if d > 0 else 0, 1)
-
-    spill_sent = []
-    for n, dx in enumerate((-1, 1)):
-        source = u2.at[:, pl.ds(FX + nx if dx > 0 else FX - 2, 2), pl.ds(PAD, ny), :]
-        spill_sent.append(send(source, xr.at[n], (dx, 0, 0)))
-    for n, dy in enumerate((-1, 1)):
-        spill_sent.append(send(ys.at[n], yr.at[n], (0, dy, 0)))
-    for n, d in enumerate(corners):
-        spill_sent.append(send(xe.at[n], xer.at[n], d))
-    for n, (dx, dy, dz) in enumerate(SPILL_Z):
-        tp, rpart = tile_part(dx), row_part(dy, 8, wide)
-        source = sp.at[tp, rpart, :]
-        spill_sent.append(send(source, spr.at[n, pl.ds(0, tp.size), pl.ds(0, rpart.size), :], (dx, dy, dz)))
-
-    def residual(X, at, mask, middle, before_x, after_x):
-        g, p = place(X)
-        inject = rotated(s2[g, pl.ds(PAD + at, block), :], lax.rem(LANES - p * FINE_SLOT, LANES))
-        keep_edges(e2, X, at, middle)
-        sums = near(u2, X, at, middle, before_x, after_x, inject)
-        factor = plane_mask(X)
-        if mask is not None:
-            factor = factor * mask
-        return [(f[t, X, pl.ds(at + 4, block), :] - 6.0 * middle[t] + sums[t]) * factor for t in range(nt)]
-
-    for at, mask in zip(blocks, row_masks):
-        def step_x(i, carry, at=at, mask=mask):
-            before_x, middle, part = carry
-            X = FX + 2 * i - 3
-            after_x = plane_of(u2, X + 1, at)
-            beyond = plane_of(u2, X + 2, at)
-            odd = residual(X, at, mask, middle, before_x, after_x)
-            even = residual(X + 1, at, mask, after_x, middle, beyond)
-            quarter = [0.25 * e for e in even]
-            for t in range(nt):
-                px[t, i, pl.ds(at + 4, block), :] = part[t] + 0.5 * odd[t] + quarter[t]
-            return after_x, beyond, quarter
-
-        start = (plane_of(u2, FX - 4, at), plane_of(u2, FX - 3, at), [zero_b] * nt)
-        _, _, part = unrolled(0, mx + 3, step_x, start, BYX)
-        for t in range(nt):
-            px[t, mx + 3, pl.ds(at + 4, block), :] = part[t]
-
-    for g in range(tiles):
-        here, total = sides(s2, g, rows_w, FINE_SLOT, slot_w, off_w, e2)
-        rs[g, rows_w, :] = (total - 6.0 * here) * fm[g]
+        low, high = max(0, 16 * g - 8), min(nx, 16 * g + 8)
+        for side, y in ((0, -2), (1, ny)):
+            for k in range(2):
+                for t in range(nt):
+                    ys[side, k, t, low:high] = flat[t, rows_along(y + k, low, high - low), :]
+        for n, (dx, dy, _) in enumerate(corners):
+            if g == (last_tile if dx > 0 else 0):
+                X, y = (FX + nx if dx > 0 else FX - 1), (PAD + ny if dy > 0 else PAD - 1)
+                for t in range(nt):
+                    xe[n, t:t + 1, :] = u2[t, X, y:y + 1, :]
+
+    def send_spill(g):
+        low, high = max(0, 16 * g - 8), min(nx, 16 * g + 8)
+        planes = pl.ds(low, high - low)
+        for n, dy in enumerate((-1, 1)):
+            spill_sent.append(send(ys.at[n, :, :, planes, :], yr.at[n, :, :, planes, :], (0, dy, 0)))
+        for n, (dx, dy, dz) in enumerate(SPILL_Z):
+            if dx:
+                if g == (last_tile if dx > 0 else 0):
+                    spill_sent.append(send(sp.at[pl.ds(g, 1), rows_w, :], spr.at[n, pl.ds(0, 1)], (dx, dy, dz)))
+            elif dy == 0:
+                spill_sent.append(send(sp.at[pl.ds(g, 1), rows_w, :], spr.at[n, pl.ds(g, 1)], (dx, dy, dz)))
+            elif g in (last_tile - 2, last_tile):
+                some = pl.ds(0, g + 1) if g < last_tile else pl.ds(g - 1, 2)
+                rows = row_part(dy, PAD, wide)
+                spill_sent.append(send(sp.at[some, rows, :], spr.at[n, some, pl.ds(0, PAD), :], (dx, dy, dz)))
+        for n, d in enumerate(corners):
+            if g == (last_tile if d[0] > 0 else 0):
+                spill_sent.append(send(xe.at[n], xer.at[n], d))
+        for n, dx in enumerate((-1, 1)):
+            if g == (last_tile if dx > 0 else 0):
+                source = u2.at[:, pl.ds(FX + nx if dx > 0 else FX - 2, 2), pl.ds(PAD, ny), :]
+                spill_sent.append(send(source, xr.at[n], (dx, 0, 0)))
 
     quarter, half = 0.25 * STEP, 0.5 * STEP
 
@@ -411,7 +467,6 @@
             py[i, :, t * LANES:(t + 1) * LANES] = quarter * (evens + nexts) + half * odds
         return 0
 
-    unrolled(0, mx + 4, step_y, 0, 4)
 
     def weights(gap, scale):
         outer = jnp.logical_or(gap == 0, gap == 2)
@@ -437,25 +492,24 @@
     pack_strip = weights(p_of - 2 * q_of, 1.0) * weights(zf_of - 2 * kk_of, 1.0)
     pack_strip = jnp.where(used, pack_strip, 0.0).astype(jnp.bfloat16)
 
-    group = 4 if (mx + 4) % 4 == 0 else 1
     lane_c = iota((rows_c, LANES), 1)
     slot_c, off_c = slots(lane_c, COARSE_SLOT)
     rows_m = pl.ds(PAD, rows_c)
 
     def place_c(index):
-        return lax.div(index, 8), lax.rem(index, 8)
+        return divide(index, 8)
+
+    pack = 4 if (mx + 4) % 4 == 0 else 1
 
     def step_z(j, _):
-        both = split_dot(py[pl.ds(j * group, group)].reshape(group * rows_c, nz), down)
-        both = both.reshape(group, rows_c, 2 * LANES)
-        for n in range(group):
-            index = j * group + n + 2
+        both = split_dot(py[pl.ds(j * pack, pack)].reshape(pack * rows_c, nz), down)
+        both = both.reshape(pack, rows_c, 2 * LANES)
+        for n in range(pack):
+            index = j * pack + n + 2
             mp[index, rows_m, :] = both[n, :, :LANES]
             g, q = place_c(index)
             pltpu.store(pk.at[g, rows_m, :], rotated(both[n, :, LANES:], q * COARSE_SLOT), mask=slot_c == q)
         return 0
-
-    unrolled(0, (mx + 4) // group, step_z, 0, 3)
 
     def strip_y(g):
         start = SR - 8
@@ -464,72 +518,133 @@
         nexts = rs[g, pl.ds(start + 2, rows_c, stride=2), :]
         return quarter * (evens + nexts) + half * odds
 
-    parts = [strip_y(g) for g in range(tiles)] + [jnp.zeros((rows_c, LANES), f32)]
-    for g in range(tiles):
-        pk[g, rows_m, :] += split_dot(jnp.concatenate(parts[g:g + 2], 1), pack_strip)
-
-    def plane_part(dx):
-        if dx == 0:
-            return pl.ds(2, mx + 4)
-        return pl.ds(mx, 6) if dx > 0 else pl.ds(2, 5)
-
-    waits_m, waits_p = {}, {}
-    for n, d in enumerate(PLANAR):
-        planes, rows = plane_part(d[0]), row_part(d[1], PAD, rows_c)
-        target = rm.at[n, pl.ds(0, planes.size), pl.ds(0, rows.size), :]
-        waits_m[d] = send(mp.at[planes, rows, :], target, d)
-    for n, d in enumerate(NEIGHBOURS):
-        tp, rows = tile_part(d[0]), row_part(d[1], PAD, rows_c)
-        if d[0] == 0:
-            target = rp.at[(d[1] + 1) * 3 + d[2] + 1, :, pl.ds(0, rows.size), :]
-        else:
-            target = rpx.at[n, :, pl.ds(0, rows.size), :]
-        waits_p[d] = send(pk.at[tp, rows, :], target, d)
-
-    for number in spill_sent:
-        arrive(number)
+    def strips_pack(g):
+        beyond = strip_y(g + 1) if g + 1 < tiles else jnp.zeros((rows_c, LANES), f32)
+        pk[g, rows_m, :] += split_dot(jnp.concatenate([strip_y(g), beyond], 1), pack_strip)
+
+    def send_planes(first, last):
+        for n, d in enumerate(PLANAR):
+            rows = row_part(d[1], PAD, rows_c)
+            if d[0] == 0:
+                planes, target = pl.ds(first, last - first), pl.ds(first - 2, last - first)
+            elif (last == mx + 6) if d[0] > 0 else (first == 2):
+                planes, target = (pl.ds(mx, 6), pl.ds(0, 6)) if d[0] > 0 else (pl.ds(2, 5), pl.ds(0, 5))
+            else:
+                continue
+            waits_m.append(send(mp.at[planes, rows, :], rm.at[n, target, pl.ds(0, rows.size), :], d))
+
+    def send_strips(first, last):
+        final = last == tiles
+        for side in range(2):
+            for g in range(first, last, 2):
+                value = pk[g, rows_m, :]
+                if g + 1 < tiles:
+                    keep = off_c >= 0 if side else off_c < 0
+                    value = jnp.where(keep, value, rotated(pk[g + 1, rows_m, :], -8 if side else 8))
+                pz[side, g // 2, rows_m, :] = value
+        pairs = pl.ds(first // 2, (last + 1) // 2 - first // 2)
+        for n, d in enumerate(NEIGHBOURS):
+            rows = row_part(d[1], PAD, rows_c)
+            if d[0]:
+                if (d[0] > 0) == final:
+                    target = rpx.at[n, :, pl.ds(0, rows.size), :]
+                    waits_p.append(send(pk.at[pl.ds(last_tile if final else 0, 1), rows, :], target, d))
+                continue
+            some = pairs if d[2] else pl.ds(first, last - first)
+            source = pz.at[int(d[2] > 0), some, rows, :] if d[2] else pk.at[some, rows, :]
+            target = rp.at[(d[1] + 1) * 3 + d[2] + 1, some, pl.ds(0, rows.size), :]
+            waits_p.append(send(source, target, d))
+
+    carries = [[zero_b] * nt for _ in blocks]
+
+    def restrict_part(first, last, first_g, last_g):
+        for g in range(first_g, min(last_g + 1, tiles)):
+            here, total = sides(s2, g, rows_w, FINE_SLOT, slot_w, off_w, e2)
+            rs[g, rows_w, :] = (total - 6.0 * here) * fm[g]
+        unrolled(first, last, step_y, 0, 4)
+        unrolled(first // pack, last // pack, step_z, 0, BYP)
+        at_first = len(sent)
+        send_planes(first + 2, last + 2)
+        for g in range(first_g, last_g):
+            strips_pack(g)
+        send_strips(first_g, last_g)
+        start(range(at_first, len(sent)))
+
+    for c in range(chunks):
+        for load in loads[c * 2 * nt:(c + 1) * 2 * nt]:
+            load.wait()
+        final = c == chunks - 1
+        low, high = 16 * c, (nx + 1 if final else 16 * c + 15)
+        sweep(u0, u1, FX + low - 1, FX + high, e0)
+        sweep(u1, u2, FX + low - 2, FX + (high + 1 if final else high - 1), e1, u0)
+        strips_1(c)
+        strips_1(c + 1)
+        for g in range(c, tiles if final else c + 1):
+            strips_2(g)
+            pack_spill(g)
+        if not final:
+            if c == 0:
+                pl.semaphore_wait(barrier, expected)
+            at_first = len(sent)
+            send_spill(c)
+            start(range(at_first, len(sent)))
+        carries = restrict_x(max(0, 8 * c - 3), mx + 3 if final else 8 * c + 5, carries)
+        if c == chunks - 2:
+            ready = (8 * c + 5) // pack * pack
+            whole = (ready + 2) // 16 * 2
+            restrict_part(0, ready, 0, whole)
+    for at, mask, part in zip(blocks, row_masks, carries):
+        for t in range(nt):
+            px[t, mx + 3, pl.ds(at + 4, block), :] = part[t] if mask is None else part[t] * mask
+    restrict_part(ready, mx + 4, whole, tiles)
+    at_first, early = len(sent), len(spill_sent)
+    for g in (last_tile - 1, last_tile):
+        send_spill(g)
+    start(range(at_first, len(sent)))
+
     lane_n = iota((ny, LANES), 1)
-    _, off_n = slots(lane_n, FINE_SLOT)
-    for n, X in enumerate((FX + nx - 2, FX)):
+    low_lanes, high_lanes = lane_n < 2, lane_n >= LANES - 2
+    at_z = {d: n for n, d in enumerate(SPILL_Z)}
+    rest = 16 * last_tile - 24
+
+    def add_spills(late):
+        arrive(spill_sent[early:] if late else spill_sent[:early])
+        n, X = (1, FX) if late else (0, FX + nx - 2)
         for k in range(2):
             for t in range(nt):
                 u2[t, X + k, pl.ds(PAD, ny), :] += xr[n, t, k]
-    for n, y in enumerate((ny - 2, 0)):
-        for k in range(2):
-            for t in range(nt):
-                flat[t, rows_along(y + k), :] += yr[n, k, t]
-    for n, (dx, dy, _) in enumerate(corners):
-        X, y = (FX if dx > 0 else FX + nx - 1), (PAD if dy > 0 else PAD + ny - 1)
-        for t in range(nt):
-            u2[t, X, y:y + 1, :] += xer[n, t:t + 1, :]
-    at_z = {d: n for n, d in enumerate(SPILL_Z)}
-    sums = {}
-    for dz in (-1, 1):
-        main = at_z[(0, 0, dz)]
-        for dx in (-1, 1):
-            spr[main, tiles - 1 if dx < 0 else 0] += spr[at_z[(dx, 0, dz)], 0]
-        for dy in (-1, 1):
-            row = 0 if dy > 0 else wide - PAD
-            for g in range(tiles):
-                spr[main, g, row:row + PAD] += spr[at_z[(0, dy, dz)], g, 0:PAD]
-    for g in range(tiles):
-        sp_off = off_w >= 0
-        s1[g, rows_w, :] = jnp.where(sp_off, spr[at_z[(0, 0, 1)], g], spr[at_z[(0, 0, -1)], g])
-    low_lanes, high_lanes = lane_n < 2, lane_n >= LANES - 2
-
-    def add_z(x, _):
-        g, p = place(x + FX)
-        value = rotated(s1[g, pl.ds(SR, ny), :], lax.rem(LANES - p * FINE_SLOT, LANES))
-        u2[0, x + FX, pl.ds(PAD, ny), :] += jnp.where(low_lanes, value, 0.0)
-        u2[nt - 1, x + FX, pl.ds(PAD, ny), :] += jnp.where(high_lanes, value, 0.0)
-        return 0
-
-    unrolled(0, nx, add_z, 0, BYZ)
-
-    for d in PLANAR:
-        arrive(waits_m[d])
-    for d in NEIGHBOURS:
-        arrive(waits_p[d])
+        first, count = (rest, nx - rest) if late else (0, rest)
+        for n, y in enumerate((ny - 2, 0)):
+            for k in range(2):
+                for t in range(nt):
+                    flat[t, rows_along(y + k, first, count), :] += yr[n, k, t, first:first + count]
+        for n, (dx, dy, _) in enumerate(corners):
+            if (dx > 0) == late:
+                X, y = (FX if dx > 0 else FX + nx - 1), (PAD if dy > 0 else PAD + ny - 1)
+                for t in range(nt):
+                    u2[t, X, y:y + 1, :] += xer[n, t:t + 1, :]
+        some = (0, last_tile - 1, last_tile) if late else range(1, last_tile - 1)
+        for g in some:
+            parts = []
+            for dz in (1, -1):
+                pieces = [spr[at_z[(0, 0, dz)], g]]
+                for dx in (-1, 1):
+                    if g == (last_tile if dx < 0 else 0):
+                        pieces.append(spr[at_z[(dx, 0, dz)], 0])
+                part = sum(pieces[1:], pieces[0])
+                top = part[0:PAD] + spr[at_z[(0, 1, dz)], g, 0:PAD]
+                end = part[wide - PAD:] + spr[at_z[(0, -1, dz)], g, 0:PAD]
+                parts.append(jnp.concatenate([top, part[PAD:wide - PAD], end], 0))
+            s1[g, rows_w, :] = jnp.where(off_w >= 0, parts[0], parts[1])
+            for x in range(max(0, 16 * g - 8), min(nx, 16 * g + 8)):
+                p = divide(x + 8, 16)[1]
+                value = turned_back(s1[g, pl.ds(SR, ny), :], p * FINE_SLOT)
+                u2[0, x + FX, pl.ds(PAD, ny), :] += jnp.where(low_lanes, value, 0.0)
+                u2[nt - 1, x + FX, pl.ds(PAD, ny), :] += jnp.where(high_lanes, value, 0.0)
+
+    add_spills(False)
+
+    arrive(waits_m + waits_p)
     at_p = {d: n for n, d in enumerate(NEIGHBOURS)}
     at_m = {d: n for n, d in enumerate(PLANAR)}
     last = rows_c - PAD
@@ -540,22 +655,24 @@
     pieces = {}
     for dz in SIDES:
         for g in range(tiles):
-            base = pk[g, rows_m, :] if dz == 0 else rp[3 + dz + 1, g]
-            pieces[dz, g] = [base[r:r + PAD] for r in range(0, rows_c, PAD)]
+            at = g if dz == 0 else g // 2
+            base = pk[g, rows_m, :] if dz == 0 else rp[3 + dz + 1, at]
+            parts = [base[r:r + PAD] for r in range(0, rows_c, PAD)]
             for dy in (-1, 1):
-                extra = rp[(dy + 1) * 3 + dz + 1, g, 0:PAD]
-                pieces[dz, g][row_at(dy) // PAD] += extra
-        for dx in (-1, 1):
-            g = 0 if dx > 0 else tiles - 1
-            for dy in SIDES:
-                ref = rpx.at[at_p[(dx, dy, dz)], 0]
-                if dy == 0:
-                    for n in range(rows_c // PAD):
-                        pieces[dz, g][n] += ref[n * PAD:(n + 1) * PAD]
-                else:
-                    pieces[dz, g][row_at(dy) // PAD] += ref[0:PAD]
+                parts[row_at(dy) // PAD] += rp[(dy + 1) * 3 + dz + 1, at, 0:PAD]
+            if g in (0, last_tile):
+                dx = -1 if g else 1
+                for dy in SIDES:
+                    ref = rpx.at[at_p[(dx, dy, dz)], 0]
+                    if dy == 0:
+                        for n in range(rows_c // PAD):
+                            parts[n] += ref[n * PAD:(n + 1) * PAD]
+                    else:
+                        parts[row_at(dy) // PAD] += ref[0:PAD]
+            whole_rows = jnp.concatenate(parts, 0)
+            pieces[dz, g] = rotated(whole_rows, 8 * dz) if dz and g % 2 else whole_rows
     for g in range(tiles):
-        own, low, high = (jnp.concatenate(pieces[dz, g], 0) for dz in (0, 1, -1))
+        own, low, high = (pieces[dz, g] for dz in (0, 1, -1))
         value = jnp.where(jnp.logical_and(off_c >= -2, off_c <= 1), own, 0.0)
         value = value + jnp.where(off_c >= 0, rotated(low, LANES - 4), rotated(high, 3))
         d0[g, rows_m, :] = value * em[g]
@@ -572,7 +689,7 @@
     def build(index, extra=None):
         g, q = place_c(index)
         here = mp[index, rows_m, :] if extra is None else extra
-        value = here + jnp.where(near_c, rotated(ad[g], lax.rem(LANES - q * COARSE_SLOT, LANES)), 0.0)
+        value = here + jnp.where(near_c, turned_back(ad[g], q * COARSE_SLOT), 0.0)
         value = value * (kc[...] * plane_mask_c(index))
         c0[index, rows_m, :] = value
 
@@ -606,7 +723,7 @@
 
         def sweep_c(index, _, old=old, new=new, k=k):
             g, q = place_c(index)
-            inject = rotated(strips[k][g, rows_m, :], lax.rem(LANES - q * COARSE_SLOT, LANES))
+            inject = turned_back(strips[k][g, rows_m, :], q * COARSE_SLOT)
             here = old[index, rows_m, :]
             total = here + old[index - 1, rows_m, :] + old[index + 1, rows_m, :]
             total = total + old[index, pl.ds(PAD - 1, rows_c), :] + old[index, pl.ds(PAD + 1, rows_c), :]
@@ -622,6 +739,8 @@
             here, total = sides(strips[k], g, rows_m, COARSE_SLOT, slot_c, off_c, touch[k])
             strips[k + 1][g, rows_m, :] = (here + total) * (em[g] * (0.25 * STEP)) + d0[g, rows_m, :]
 
+    add_spills(True)
+
     up = weights(iota((mz, nz), 1) - 2 * iota((mz, nz), 0), 2.0).astype(jnp.bfloat16)
     three = 3 if (mx + 1) % 3 == 0 else 1
 
@@ -629,7 +748,7 @@
         value = split_dot(c3[pl.ds(3 + j * three, three), rows_m, :].reshape(three * rows_c, LANES), up)
         for n in range(three):
             g, q = place_c(3 + j * three + n)
-            outside = 0.5 * rotated(d3[g, rows_m, :], lax.rem(LANES - q * COARSE_SLOT, LANES))
+            outside = 0.5 * turned_back(d3[g, rows_m, :], q * COARSE_SLOT)
             for t in range(nt):
                 part = value[n * rows_c:(n + 1) * rows_c, t * LANES:(t + 1) * LANES]
                 if t == 0:
@@ -639,10 +758,11 @@
 
     unrolled(0, (mx + 1) // three, prolong_z, 0, 3)
 
-    for copy, d, _ in sent:
+    for d, some in by_direction(range(len(sent))):
         @pl.when(there(d))
-        def _(copy=copy, d=d):
-            copy(d).wait_send()
+        def _(d=d, some=some):
+            for number in some:
+                sent[number][0](d).wait_send()
 
 
 def add_kernel(per, smooth_ref, q_ref, out_hbm, both, out_ref, sems):
@@ -708,12 +828,13 @@
             strip, strip, strip, strip, strip, strip,
             strip, vm(len(SPILL_Z), tiles, ny + PAD, LANES), vm(tiles, ny + PAD, LANES),
             vm(2, 2, nt, nx, LANES), vm(2, 2, nt, nx, LANES), vm(2, nt, 2, ny, LANES), vm(4, PAD, LANES), vm(4, PAD, LANES),
-            coarse, strip_c, vm(tiles, my + PAD, LANES), vm(my + PAD, LANES),
+            coarse, strip_c, vm(2, (tiles + 1) // 2, my + 3 * PAD, LANES),
+            vm(tiles, my + PAD, LANES), vm(my + PAD, LANES),
             vm(len(PLANAR), mx + 4, my + PAD, LANES), vm(9, tiles, my + PAD, LANES),
             vm(len(NEIGHBOURS), 1, my + PAD, LANES),
             coarse, coarse, coarse, coarse, strip_c, strip_c, strip_c, strip_c, strip_c, strip_c, strip_c,
             vm(tiles, my + PAD, LANES),
-            pltpu.SemaphoreType.DMA((8 * nt,)),
+            pltpu.SemaphoreType.DMA((2 * nt * tiles,)),
             pltpu.SemaphoreType.DMA((N_COPIES,)),
             pltpu.SemaphoreType.DMA((N_COPIES,)),
         ],

time: 38.1 us -> 33 us (0.87)
  Pallas kernels: 37.9 us -> 32.6 us
    pallas_call x1, Pallas kernels: 35.7 us -> 30.4 us  [on_device(): pl.pallas_call(functools.partial(correct_kernel, sizes), out_shape=(pltpu...]
where the time goes in v3:
time: 33 us; the launch traced here: 32.8 us
  Pallas kernels  32.6 us (99%)
    pallas_call x1, Pallas kernels, on_device(): pl.pallas_call(functools.partial(correct_kernel, sizes), out_shape=(pltpu...  30.4 us
    pallas_call x1, Pallas kernels, on_device(): pl.pallas_call(functools.partial(add_kernel, per), out_shape=jax.ShapeDty...  2.25 us

profile of v3, /device:TPU:0, one launch (start us, length us, event | category | flops | bytes accessed | tf_op | source)
XLA Modules:
  0.0 32.8 jit_solution(705063971449825630)
XLA Ops:
  0.0 30.4 %shard_map.28 = (f32[2,72,80,128]{3,2,1,0:T(8,128)S(1)}, f32[33,2,40,128]{3,2,1,0:T(8,128)S(1)}) custom-call(f32[64,64,256]{2,1,0:T(8,128)} %start_hbm.1, f32[64,64,256]{2,1,0:T(8,128)} %right_hbm.1), custom_call_target="tpu_custom_call" | custom-call | tf_op jit(solution)/shard_map/pallas_call | solution.py:817
  30.4 2.2 %shard_map.29 = f32[64,64,256]{2,1,0:T(8,128)} custom-call(f32[2,72,80,128]{3,2,1,0:T(8,128)S(1)} %get-tuple-element.7.smooth_ref, f32[33,2,40,128]{3,2,1,0:T(8,128)S(1)} %get-tuple-element.8.q_ref), custom_call_target="tpu_custom_call" | custom-call | tf_op jit(solution)/shard_map/pallas_call | solution.py:845

commit v4 on v3

--- a/solution.py
+++ b/solution.py
@@ -14,7 +14,7 @@
 BY = 20
 BYX = 14
 BYC = 40
-BYP = 3
+BYP = 5
 BYZ = 8
 LANES = 128
 PAD = 8
@@ -582,12 +582,14 @@
         for g in range(c, tiles if final else c + 1):
             strips_2(g)
             pack_spill(g)
-        if not final:
-            if c == 0:
-                pl.semaphore_wait(barrier, expected)
-            at_first = len(sent)
-            send_spill(c)
-            start(range(at_first, len(sent)))
+        if c == 0:
+            pl.semaphore_wait(barrier, expected)
+        at_first = len(sent)
+        if final:
+            early = len(spill_sent)
+        for g in range(c, tiles if final else c + 1):
+            send_spill(g)
+        start(range(at_first, len(sent)))
         carries = restrict_x(max(0, 8 * c - 3), mx + 3 if final else 8 * c + 5, carries)
         if c == chunks - 2:
             ready = (8 * c + 5) // pack * pack
@@ -597,11 +599,6 @@
         for t in range(nt):
             px[t, mx + 3, pl.ds(at + 4, block), :] = part[t] if mask is None else part[t] * mask
     restrict_part(ready, mx + 4, whole, tiles)
-    at_first, early = len(sent), len(spill_sent)
-    for g in (last_tile - 1, last_tile):
-        send_spill(g)
-    start(range(at_first, len(sent)))
-
     lane_n = iota((ny, LANES), 1)
     low_lanes, high_lanes = lane_n < 2, lane_n >= LANES - 2
     at_z = {d: n for n, d in enumerate(SPILL_Z)}
@@ -643,6 +640,7 @@
                 u2[nt - 1, x + FX, pl.ds(PAD, ny), :] += jnp.where(high_lanes, value, 0.0)
 
     add_spills(False)
+    add_spills(True)
 
     arrive(waits_m + waits_p)
     at_p = {d: n for n, d in enumerate(NEIGHBOURS)}
@@ -738,8 +736,6 @@
         for g in range(tiles):
             here, total = sides(strips[k], g, rows_m, COARSE_SLOT, slot_c, off_c, touch[k])
             strips[k + 1][g, rows_m, :] = (here + total) * (em[g] * (0.25 * STEP)) + d0[g, rows_m, :]
-
-    add_spills(True)
 
     up = weights(iota((mz, nz), 1) - 2 * iota((mz, nz), 0), 2.0).astype(jnp.bfloat16)
     three = 3 if (mx + 1) % 3 == 0 else 1

time: 33 us -> 32.5 us (0.985)
  Pallas kernels: 32.6 us -> 32.2 us
    pallas_call x1, Pallas kernels: 30.4 us -> 29.9 us  [on_device(): pl.pallas_call(functools.partial(correct_kernel, sizes), out_shape=(pltpu...]
where the time goes in v4:
time: 32.5 us; the launch traced here: 32.4 us
  Pallas kernels  32.2 us (99%)
    pallas_call x1, Pallas kernels, on_device(): pl.pallas_call(functools.partial(correct_kernel, sizes), out_shape=(pltpu...  29.9 us
    pallas_call x1, Pallas kernels, on_device(): pl.pallas_call(functools.partial(add_kernel, per), out_shape=jax.ShapeDty...  2.25 us

profile of v4, /device:TPU:0, one launch (start us, length us, event | category | flops | bytes accessed | tf_op | source)
XLA Modules:
  0.0 32.4 jit_solution(16420057653839376164)
XLA Ops:
  0.0 29.9 %shard_map.28 = (f32[2,72,80,128]{3,2,1,0:T(8,128)S(1)}, f32[33,2,40,128]{3,2,1,0:T(8,128)S(1)}) custom-call(f32[64,64,256]{2,1,0:T(8,128)} %start_hbm.1, f32[64,64,256]{2,1,0:T(8,128)} %right_hbm.1), custom_call_target="tpu_custom_call" | custom-call | tf_op jit(solution)/shard_map/pallas_call | solution.py:813
  30.0 2.2 %shard_map.29 = f32[64,64,256]{2,1,0:T(8,128)} custom-call(f32[2,72,80,128]{3,2,1,0:T(8,128)S(1)} %get-tuple-element.7.smooth_ref, f32[33,2,40,128]{3,2,1,0:T(8,128)S(1)} %get-tuple-element.8.q_ref), custom_call_target="tpu_custom_call" | custom-call | tf_op jit(solution)/shard_map/pallas_call | solution.py:841
